TPU v7x, 256 devices: a whole 4x4x8 slice. The times are simulated.
256 devices in a mesh: ka: 64 (over z, x, y_lo), orb: 4 (over y_hi, core).
Axes of the slice: x: 4, y: 4 (y_hi: 2, y_lo: 2; y = y_hi * 2 + y_lo), z: 8, core: 2. Of those that a mesh axis runs over, the one named last changes fastest.
Arguments:
- fock: float32 [2, 256, 384, 384], P(None, 'ka', 'orb'), may hold values from -3 to 3, as said below
- potential: float32 [4, 48, 48], P(None, 'orb'), may hold values from -0.9 to 0.9
- chem_potential: float32 [1], replicated, may hold values from -1 to 1
- spectral_bound: float32 [1], replicated, may hold values from 5.5 to 8
- impurity_orbitals: int32 [384], replicated, may hold values from 0 to 383, each once
- potential_of: int32 [8], replicated, may hold values from 0 to 3
Outputs:
- density_cells: float32 [2, 256, 384, 384], P(None, 'ka', 'orb')
- fragment_density: float32 [2, 8, 48, 48], P(None, 'orb')
Inputs may be any that keep to these rules, and one draw needn't show every extreme that they name: `impurity_orbitals`: every orbital appears once; entries f * 48 to (f + 1) * 48 - 1 are fragment f's orbitals. `fock`: for each k-point the real part is symmetric and the imaginary part antisymmetric.
All inputs are finite; a program needn't handle non-finite values.
Results may differ from a plain program's by a relative error of at most 0.0001.
Values sent between devices are 32-bit elements; how exact they have to be, the bound alone decides.
A program may use at most 64 MiB of HBM per device.

v0:
```python
import functools
import math

import jax
import jax.numpy as jnp
import numpy as np
from jax import lax
from jax.experimental import pallas as pl
from jax.experimental.pallas import tpu as pltpu
from jax.sharding import PartitionSpec as P

ITERS = 2
N = 384
K = 256
F32 = jnp.float32
BF16 = jnp.bfloat16
MESH = pl.DeviceIdType.MESH


def split2(x):
    hi = x.astype(BF16)
    return hi, (x - hi.astype(F32)).astype(BF16)


def dot(a, b):
    return jnp.dot(a, b, preferred_element_type=F32)


def dot3(a_hi, a_lo, b_hi, b_lo):
    return dot(a_hi, b_hi) + (dot(a_hi, b_lo) + dot(a_lo, b_hi))


def contract(a, b, dims):
    return lax.dot_general(
        a, b, (dims, ((), ())), precision=lax.Precision.HIGHEST, preferred_element_type=F32
    )


def iota(shape, dim):
    return lax.broadcasted_iota(jnp.int32, shape, dim)


def remote(src, dst, send, recv, ka, orb):
    return pltpu.make_async_remote_copy(
        src_ref=src, dst_ref=dst, send_sem=send, recv_sem=recv, device_id=(ka, orb), device_id_type=MESH
    )


def wait_bytes(ref, sem):
    pltpu.make_async_copy(ref, ref, sem).wait()


def tile_of(ka, yh):
    g = ka // 36
    return (3 - 3 * g) * (1 - yh) + (1 + g) * yh, ka - 36 * g


def frag_device(o, rt):
    far = (o % 3 == 0).astype(jnp.int32)
    odd = o // 2
    h = rt * 2 + odd
    z = h % 8
    return z * 8 + (z + 1 + 3 * (h // 8)) % 8, 2 * far


def kernel(
    fock, pot, chem, bound, imp, imp4, pof, t_hi, t_lo,
    cells, frag,
    m_src, m_all, pot_all, u_ref, w_hi, w_lo, x_ref, d_tiles, k_buf, o_buf, d0_buf, f_out, f_in,
    s_fock, r_fock, s_pot, r_pot, s_k, r_k, s_o, r_o, s_d0, r_d0, s_f, r_f,
):
    ka = lax.axis_index("ka")
    orb = lax.axis_index("orb")
    z, x, yl = ka // 8, (ka // 2) % 4, ka % 2
    yh, core = orb // 2, orb % 2
    me = ka * 4 + orb

    m_src[...] = fock[0] + fock[1]
    for step in (2, 3, 1):
        to = (orb + step) % 4
        remote(pot, pot_all.at[orb], s_pot.at[step], r_pot.at[step], ka, to).start()
    for step in (2, 3, 1):
        to = (orb + step) % 4
        remote(m_src.at[to], m_all.at[orb], s_fock.at[step], r_fock.at[step], ka, to).start()
    pot_all[orb] = pot[...]
    m_all[orb] = m_src[orb]

    for step in (1, 2, 3):
        remote(pot, pot_all.at[(orb + 4 - step) % 4], s_pot.at[step], r_pot.at[step], ka, orb).wait_recv()
    slot_of = iota((N, 192), 0)
    col_of = iota((N, 192), 1)
    frag_of = slot_of // 48
    pot_of = jnp.zeros((N, 192), jnp.int32)
    for f in range(8):
        pot_of = jnp.where(frag_of == f, pof[f], pot_of)
    pick = ((col_of % 4 == pot_of) & (col_of // 4 == slot_of - 48 * frag_of)).astype(F32)
    stacked = contract(pick, pot_all[...].reshape(192, 48), ((1,), (0,)))
    spread = (iota((48, N), 1) % 48 == iota((48, N), 0)).astype(F32)
    wide = contract(stacked, spread, ((1,), (0,)))
    rows, cols = iota((N, N), 0), iota((N, N), 1)
    wide = jnp.where(rows // 48 == cols // 48, wide, 0.0)
    wide = 0.5 * (wide + wide.T)
    place = (rows == imp[...]).astype(F32)
    u_ref[...] = contract(contract(place, wide, ((1,), (0,))), place, ((1,), (1,)))

    for step in (1, 2, 3):
        remote(
            m_src.at[0], m_all.at[(orb + 4 - step) % 4], s_fock.at[step], r_fock.at[step], ka, orb
        ).wait_recv()
    m = m_all[...].reshape(N, N)
    mt = m.T
    scale = 1.0 / bound[0]
    eye = (rows == cols).astype(F32)
    x_ref[:, :N] = (0.5 * (m + mt) + u_ref[...] - chem[0] * eye) * scale
    x_ref[:, N:] = (0.5 * (m - mt)) * scale
    for step in range(ITERS):
        hi, lo = split2(x_ref[...])
        for part, w in ((hi, w_hi), (lo, w_lo)):
            w[:N, :N] = part[:, :N]
            w[:N, N:] = part[:, N:]
            w[N:, :N] = -part[:, N:]
            w[N:, N:] = part[:, :N]
        s = dot3(hi, lo, w_hi[...], w_lo[...])
        s_hi, s_lo = split2(s)
        c = dot3(s_hi, s_lo, w_hi[...], w_lo[...])
        x_ref[...] = 1.5 * x_ref[...] - 0.5 * c
    eye_half = 0.5 * eye
    for part in range(2):
        for cb in range(3):
            value = -0.5 * x_ref[:, part * N + cb * 128 : part * N + cb * 128 + 128]
            if part == 0:
                value = value + eye_half[:, cb * 128 : cb * 128 + 128]
            value = value.reshape(4, 12, 8, 128)
            for o in range(4):
                base = o * 36 + cb * 12
                d_tiles[base : base + 12, part] = value[o]

    own_o, own_j = tile_of(ka, yh)
    extra = (core == 0) & (ka == 9 * z)
    has_tile = (core == 1) | extra
    t_o = jnp.where(core == 1, own_o, 2 - 2 * yh + 0)
    t_o = jnp.where(core == 1, own_o, jnp.where(yh == 1, 0, 2))
    t_j = jnp.where(core == 1, own_j, 28 + z)

    def send_k(tile, to_ka, to_orb):
        remote(d_tiles.at[tile], k_buf.at[me], s_k, r_k, to_ka, to_orb).start()

    def spread_k(d, carry):
        to_z = (z + d % 8) % 8
        to_x = (x + (d // 8) % 4) % 4
        to_yl = (yl + (d // 32) % 2) % 2
        to_yh = (yh + d // 64) % 2
        to_ka = to_z * 8 + to_x * 2 + to_yl
        o, j = tile_of(to_ka, to_yh)

        @pl.when((d > 0) | (core == 0))
        def _():
            send_k(o * 36 + j, to_ka, to_yh * 2 + 1)

        return carry

    lax.fori_loop(0, 128, spread_k, 0)

    def spread_extra(d, carry):
        to_z = (z + d % 8) % 8
        to_yh = (yh + d // 8) % 2
        o = 2 - 2 * to_yh

        @pl.when((d > 0) | jnp.logical_not(extra))
        def _():
            send_k(o * 36 + 28 + to_z, 9 * to_z, to_yh * 2)

        return carry

    lax.fori_loop(0, 16, spread_extra, 0)

    row, cb = t_j % 12, t_j // 12

    @pl.when(has_tile)
    def _():
        k_buf[me] = d_tiles[t_o * 36 + t_j]
        wait_bytes(k_buf.at[pl.ds(0, K - 1)], r_k)
        k_rows = k_buf.reshape(K * 16, 128)
        o_rows = o_buf.reshape(2 * K * 8, 128)
        for pair in range(4):
            parts = []
            for s in (2 * pair, 2 * pair + 1):
                parts.append(
                    jnp.concatenate([k_rows[pl.ds(c * 8 + s, K, stride=16), :] for c in range(2)], axis=0)
                )
            v_hi, v_lo = split2(jnp.concatenate(parts, axis=1))
            res = dot3(t_hi[...], t_lo[...], v_hi, v_lo)
            for n, s in enumerate((2 * pair, 2 * pair + 1)):
                for c in range(2):
                    o_rows[pl.ds(c * K * 8 + s, K, stride=8), :] = res[c * K : c * K + K, n * 128 : n * 128 + 128]

        def send_d0(g, carry):
            to_ka, to_orb = frag_device(g % 4, g // 4)
            remote(o_buf.at[:, 0], d0_buf.at[t_o * 36 + t_j], s_d0, r_d0, to_ka, to_orb).start()
            return carry

        lax.fori_loop(0, 24, send_d0, 0)

        def send_o(d, carry):
            to_z = (z + d % 8) % 8
            to_x = (x + (d // 8) % 4) % 4
            to_yl = (yl + d // 32) % 2
            to_ka = to_z * 8 + to_x * 2 + to_yl
            remote(
                o_buf.at[:, pl.ds(4 * to_ka, 4)],
                cells.at[:, :, pl.ds(pl.multiple_of(8 * row, 8), 8), pl.ds(pl.multiple_of(128 * cb, 128), 128)],
                s_o, r_o, to_ka, t_o,
            ).start()
            return carry

        lax.fori_loop(0, 64, send_o, 0)

    turn = (ka % 8 + 8 - z) % 8
    makes = (core == 0) & ((turn == 1) | ((turn == 4) & (z < 4)))
    h = jnp.where(turn == 1, z, 8 + z)
    f_rt, f_odd = h // 2, h % 2
    f_o = jnp.where(yh == 1, 3 * f_odd, 1 + f_odd)

    @pl.when(makes)
    def _():
        wait_bytes(d0_buf, r_d0)
        chosen = (iota((N, 128), 0) == imp4[pl.ds(f_o, 1), :]).astype(F32)
        left = iota((48, 128), 1) < 48
        for part in range(2):
            picked = jnp.zeros((128, 128), F32)
            for cb in range(3):
                block = jnp.concatenate(
                    [d0_buf[o * 36 + cb * 12 : o * 36 + cb * 12 + 12, part].reshape(96, 128) for o in range(4)],
                    axis=0,
                )
                some = contract(chosen, block, ((0,), (0,)))
                picked = picked + contract(some, chosen[cb * 128 : cb * 128 + 128], ((1,), (0,)))
            f_out[part] = jnp.where(left, picked[:48], picked[48:96])

        def send_f(d, carry):
            to_ka = ((z + d % 8) % 8) * 8 + (ka + d // 8) % 8
            rows_at = pl.ds(pl.multiple_of(8 * f_rt, 8), 8)
            remote(f_out.at[:, rows_at], f_in.at[:, rows_at], s_f, r_f, to_ka, f_o).start()
            return carry

        lax.fori_loop(0, 64, send_f, 0)

    wait_bytes(f_in, r_f)
    for part in range(2):
        for f in range(2):
            frag[part, f] = f_in[part, :, 48 * f : 48 * f + 48]
    wait_bytes(cells, r_o)

    for step in (1, 2, 3):
        remote(pot, pot_all.at[0], s_pot.at[step], r_pot.at[step], ka, orb).wait_send()
        remote(m_src.at[0], m_all.at[0], s_fock.at[step], r_fock.at[step], ka, orb).wait_send()
    wait_bytes(d_tiles.at[pl.ds(0, 143)], s_k)

    @pl.when(jnp.logical_not(has_tile))
    def _():
        wait_bytes(d_tiles.at[0], s_k)

    @pl.when(has_tile)
    def _():
        wait_bytes(d_tiles.at[pl.ds(0, 24)], s_d0)
        wait_bytes(o_buf, s_o)

    @pl.when(makes)
    def _():
        wait_bytes(d_tiles.at[pl.ds(0, 64)], s_f)


def tables():
    grid = np.outer(np.arange(K), np.arange(K)) % K
    angle = grid * (2.0 * math.pi / K)
    c, s = np.cos(angle) / K, np.sin(angle) / K
    full = np.block([[c, -s], [s, c]]).astype(np.float32)
    hi = full.astype(jnp.bfloat16)
    lo = (full - hi.astype(np.float32)).astype(jnp.bfloat16)
    return hi, lo


def per_device(fock, potential, chem_potential, spectral_bound, impurity_orbitals, potential_of):
    t_hi, t_lo = tables()
    vmem = pl.BlockSpec(memory_space=pltpu.VMEM)
    smem = pl.BlockSpec(memory_space=pltpu.SMEM)
    dma = pltpu.SemaphoreType.DMA
    pot = potential.transpose(1, 0, 2).reshape(48, 48)
    imp4 = jnp.pad(impurity_orbitals.reshape(4, 96), ((0, 0), (0, 32)), constant_values=-1)
    return pl.pallas_call(
        kernel,
        out_shape=(
            jax.ShapeDtypeStruct((2, 4, 96, N), F32),
            jax.ShapeDtypeStruct((2, 2, 48, 48), F32),
        ),
        in_specs=[vmem, vmem, smem, smem, vmem, vmem, smem, vmem, vmem],
        out_specs=(vmem, vmem),
        scratch_shapes=[
            pltpu.VMEM((4, 96, N), F32),
            pltpu.VMEM((4, 96, N), F32),
            pltpu.VMEM((4, 48, 48), F32),
            pltpu.VMEM((N, N), F32),
            pltpu.VMEM((2 * N, 2 * N), BF16),
            pltpu.VMEM((2 * N, 2 * N), BF16),
            pltpu.VMEM((N, 2 * N), F32),
            pltpu.VMEM((144, 2, 8, 128), F32),
            pltpu.VMEM((K, 2, 8, 128), F32),
            pltpu.VMEM((2, K, 8, 128), F32),
            pltpu.VMEM((144, 2, 8, 128), F32),
            pltpu.VMEM((2, 48, 128), F32),
            pltpu.VMEM((2, 48, 128), F32),
            dma((4,)), dma((4,)), dma((4,)), dma((4,)),
            dma, dma, dma, dma, dma, dma, dma, dma,
        ],
        compiler_params=pltpu.CompilerParams(has_side_effects=True, vmem_limit_bytes=56 << 20),
        cost_estimate=pl.CostEstimate(flops=10**10, bytes_accessed=10**7, transcendentals=0),
    )(
        fock, pot, chem_potential, spectral_bound,
        impurity_orbitals.reshape(1, N), imp4, potential_of,
        jnp.asarray(t_hi), jnp.asarray(t_lo),
    )


def solution(mesh):
    return jax.shard_map(
        per_device,
        mesh=mesh,
        in_specs=(P(None, "ka", "orb", None), P(None, "orb", None), P(), P(), P(), P()),
        out_specs=(P(None, "ka", "orb", None), P(None, "orb", None, None)),
        check_vma=False,
    )
```

profile of v0, /device:TPU:24, one launch (start us, length us, event | category | flops | bytes accessed | tf_op | source)
XLA Modules:
  0.0 121.0 jit_solution(4489894436704375418)
XLA Ops:
  1.9 1.2 %reshape.14.imp = s32[1,384]{1,0:T(1,128)} reshape(s32[384]{0:T(512)} %param.12) | data formatting | bytes 3072 | tf_op jit(solution)/shard_map/reshape | solution.py:319
  3.2 0.8 reshape.15
  3.9 0.6 pad.4.imp4
  4.5 113.5 %shard_map.95 = (f32[2,4,96,384]{3,2,1,0:T(8,128)}, f32[2,2,48,48]{3,2,1,0:T(8,128)}) custom-call(f32[2,4,96,384]{3,2,1,0:T(8,128)} %fock.1, f32[48,48]{1,0:T(8,128)} %bitcast.3, f32[1]{0:T(128)S(6)} %copy.12.chem, f32[1]{0:T(128)S(6)} %copy.13.bound, s32[1,384]{1,0:T(1,128)} %reshape.14.imp, s32[4,128]{1,0:T(4,128)} %pad.4.imp4, s32[8]{0:T(128)} %pof.1, ...), custom_call_target="tpu_custom_call" | custom-call | flops 10000000000 | bytes 10000000 | tf_op jit(solution)/shard_map/pallas_call | solution.py:290
  118.0 0.0 copy-start
  118.0 2.4 %copy.14 = f32[2,4,96,384]{3,2,1,0:T(8,128)} copy(f32[2,4,96,384]{3,2,1,0:T(8,128)} %get-tuple-element.4) | data formatting | bytes 2359296
  120.4 0.0 copy-done
  120.4 0.6 copy.15
Async XLA Ops:
  118.0 2.4 %copy-start = (f32[2,2,48,48]{3,2,1,0:T(8,128)S(1)}, f32[2,2,48,48]{3,2,1,0:T(8,128)}, u32[]{:S(2)}) copy-start(f32[2,2,48,48]{3,2,1,0:T(8,128)} %get-tuple-element.5) | copy-start | bytes 110596
where the time goes:
time: 121 us
  Pallas kernels  113 us (93%)
  local copies, waits for them, and re-layouts  5.64 us (5%)
  between operations  1.94 us (2%)
    pallas_call x1, Pallas kernels, per_device(): pl.pallas_call(kernel, out_shape=(jax.ShapeDtypeStruct((2, 4, 96, N), F32...  113 us
    unnamed x4, local copies, waits for them, and re-layouts  3.05 us

commit v1 on v0

--- a/solution.py
+++ b/solution.py
@@ -63,19 +63,16 @@
     return z * 8 + (z + 1 + 3 * (h // 8)) % 8, 2 * far
 
 
-def kernel(
-    fock, pot, chem, bound, imp, imp4, pof, t_hi, t_lo,
-    cells, frag,
-    m_src, m_all, pot_all, u_ref, w_hi, w_lo, x_ref, d_tiles, k_buf, o_buf, d0_buf, f_out, f_in,
-    s_fock, r_fock, s_pot, r_pot, s_k, r_k, s_o, r_o, s_d0, r_d0, s_f, r_f,
+def gather_kernel(
+    fock, pot, chem, bound, imp, pof, x_out, m_src, m_all, pot_all, u_ref, s_fock, r_fock, s_pot, r_pot
 ):
     ka = lax.axis_index("ka")
     orb = lax.axis_index("orb")
-    z, x, yl = ka // 8, (ka // 2) % 4, ka % 2
-    yh, core = orb // 2, orb % 2
-    me = ka * 4 + orb
-
+    barrier = pltpu.get_barrier_semaphore()
+    for step in (1, 2, 3):
+        pl.semaphore_signal(barrier, inc=1, device_id=(ka, (orb + step) % 4), device_id_type=MESH)
     m_src[...] = fock[0] + fock[1]
+    pl.semaphore_wait(barrier, 3)
     for step in (2, 3, 1):
         to = (orb + step) % 4
         remote(pot, pot_all.at[orb], s_pot.at[step], r_pot.at[step], ka, to).start()
@@ -111,8 +108,37 @@
     mt = m.T
     scale = 1.0 / bound[0]
     eye = (rows == cols).astype(F32)
-    x_ref[:, :N] = (0.5 * (m + mt) + u_ref[...] - chem[0] * eye) * scale
-    x_ref[:, N:] = (0.5 * (m - mt)) * scale
+    x_out[:, :N] = (0.5 * (m + mt) + u_ref[...] - chem[0] * eye) * scale
+    x_out[:, N:] = (0.5 * (m - mt)) * scale
+    for step in (1, 2, 3):
+        remote(pot, pot_all.at[0], s_pot.at[step], r_pot.at[step], ka, orb).wait_send()
+        remote(m_src.at[0], m_all.at[0], s_fock.at[step], r_fock.at[step], ka, orb).wait_send()
+
+
+def main_kernel(
+    x_in, imp, t_hi, t_lo, cells, f_in,
+    x_ref, w_hi, w_lo, d_tiles, k_buf, o_buf, d0_buf, f_out,
+    entered, s_k, r_k, s_o, r_o, s_d0, r_d0, s_f, r_f,
+):
+    ka = lax.axis_index("ka")
+    orb = lax.axis_index("orb")
+    z, x, yl = ka // 8, (ka // 2) % 4, ka % 2
+    yh, core = orb // 2, orb % 2
+    me = ka * 4 + orb
+    barrier = pltpu.get_barrier_semaphore()
+
+    def greet(d, carry):
+        plane = (ka + d // 4) % 8
+        pl.semaphore_signal(barrier, inc=1, device_id=(8 * z + plane, (orb + d) % 4), device_id_type=MESH)
+        return carry
+
+    lax.fori_loop(1, 32, greet, 0)
+    for step in range(1, 8):
+        pl.semaphore_signal(barrier, inc=1, device_id=((ka + 8 * step) % 64, orb), device_id_type=MESH)
+
+    x_ref[...] = x_in[...]
+    rows, cols = iota((N, N), 0), iota((N, N), 1)
+    eye = (rows == cols).astype(F32)
     for step in range(ITERS):
         hi, lo = split2(x_ref[...])
         for part, w in ((hi, w_hi), (lo, w_lo)):
@@ -124,6 +150,10 @@
         s_hi, s_lo = split2(s)
         c = dot3(s_hi, s_lo, w_hi[...], w_lo[...])
         x_ref[...] = 1.5 * x_ref[...] - 0.5 * c
+        if step == 0:
+            pl.semaphore_wait(barrier, 38)
+            for hop in range(1, 8):
+                pl.semaphore_signal(entered, inc=1, device_id=((ka + 8 * hop) % 64, orb), device_id_type=MESH)
     eye_half = 0.5 * eye
     for part in range(2):
         for cb in range(3):
@@ -138,9 +168,10 @@
     own_o, own_j = tile_of(ka, yh)
     extra = (core == 0) & (ka == 9 * z)
     has_tile = (core == 1) | extra
-    t_o = jnp.where(core == 1, own_o, 2 - 2 * yh + 0)
     t_o = jnp.where(core == 1, own_o, jnp.where(yh == 1, 0, 2))
     t_j = jnp.where(core == 1, own_j, 28 + z)
+
+    pl.semaphore_wait(entered, 7)
 
     def send_k(tile, to_ka, to_orb):
         remote(d_tiles.at[tile], k_buf.at[me], s_k, r_k, to_ka, to_orb).start()
@@ -223,8 +254,13 @@
 
     @pl.when(makes)
     def _():
+        slots = [imp[:, 96 * o : 96 * o + 96] for o in range(4)]
+        own_slots = slots[0]
+        for o in range(1, 4):
+            own_slots = jnp.where(f_o == o, slots[o], own_slots)
+        own_slots = jnp.concatenate([own_slots, jnp.full((1, 32), -1, jnp.int32)], axis=1)
         wait_bytes(d0_buf, r_d0)
-        chosen = (iota((N, 128), 0) == imp4[pl.ds(f_o, 1), :]).astype(F32)
+        chosen = (iota((N, 128), 0) == own_slots).astype(F32)
         left = iota((48, 128), 1) < 48
         for part in range(2):
             picked = jnp.zeros((128, 128), F32)
@@ -246,28 +282,33 @@
         lax.fori_loop(0, 64, send_f, 0)
 
     wait_bytes(f_in, r_f)
+    wait_bytes(cells, r_o)
+
+    wait_bytes(d_tiles.at[pl.ds(0, 143)], s_k)
+
+    @pl.when(jnp.logical_not(has_tile))
+    def _():
+        wait_bytes(d_tiles.at[0], s_k)
+
+    @pl.when(has_tile)
+    def _():
+        wait_bytes(d_tiles.at[pl.ds(0, 24)], s_d0)
+        wait_bytes(o_buf, s_o)
+
+    @pl.when(makes)
+    def _():
+        wait_bytes(d_tiles.at[pl.ds(0, 64)], s_f)
+
+
+def store_kernel(cells, f_in, out, frag, sem):
+    stores = [pltpu.make_async_copy(cells.at[c], out.at[c], sem.at[c]) for c in range(2)]
+    for store in stores:
+        store.start()
     for part in range(2):
         for f in range(2):
             frag[part, f] = f_in[part, :, 48 * f : 48 * f + 48]
-    wait_bytes(cells, r_o)
-
-    for step in (1, 2, 3):
-        remote(pot, pot_all.at[0], s_pot.at[step], r_pot.at[step], ka, orb).wait_send()
-        remote(m_src.at[0], m_all.at[0], s_fock.at[step], r_fock.at[step], ka, orb).wait_send()
-    wait_bytes(d_tiles.at[pl.ds(0, 143)], s_k)
-
-    @pl.when(jnp.logical_not(has_tile))
-    def _():
-        wait_bytes(d_tiles.at[0], s_k)
-
-    @pl.when(has_tile)
-    def _():
-        wait_bytes(d_tiles.at[pl.ds(0, 24)], s_d0)
-        wait_bytes(o_buf, s_o)
-
-    @pl.when(makes)
-    def _():
-        wait_bytes(d_tiles.at[pl.ds(0, 64)], s_f)
+    for store in stores:
+        store.wait()
 
 
 def tables():
@@ -284,41 +325,63 @@
     t_hi, t_lo = tables()
     vmem = pl.BlockSpec(memory_space=pltpu.VMEM)
     smem = pl.BlockSpec(memory_space=pltpu.SMEM)
+    anywhere = pl.BlockSpec(memory_space=pl.ANY)
     dma = pltpu.SemaphoreType.DMA
     pot = potential.transpose(1, 0, 2).reshape(48, 48)
-    imp4 = jnp.pad(impurity_orbitals.reshape(4, 96), ((0, 0), (0, 32)), constant_values=-1)
-    return pl.pallas_call(
-        kernel,
-        out_shape=(
-            jax.ShapeDtypeStruct((2, 4, 96, N), F32),
-            jax.ShapeDtypeStruct((2, 2, 48, 48), F32),
-        ),
-        in_specs=[vmem, vmem, smem, smem, vmem, vmem, smem, vmem, vmem],
-        out_specs=(vmem, vmem),
+    imp = impurity_orbitals.reshape(1, N)
+    start = pl.pallas_call(
+        gather_kernel,
+        name="gather",
+        out_shape=jax.ShapeDtypeStruct((N, 2 * N), F32),
+        in_specs=[vmem, vmem, smem, smem, vmem, smem],
+        out_specs=vmem,
         scratch_shapes=[
             pltpu.VMEM((4, 96, N), F32),
             pltpu.VMEM((4, 96, N), F32),
             pltpu.VMEM((4, 48, 48), F32),
             pltpu.VMEM((N, N), F32),
+            dma((4,)), dma((4,)), dma((4,)), dma((4,)),
+        ],
+        compiler_params=pltpu.CompilerParams(
+            has_side_effects=True, collective_id=0, vmem_limit_bytes=40 << 20
+        ),
+    )(fock, pot, chem_potential, spectral_bound, imp, potential_of)
+    cells, f_in = pl.pallas_call(
+        main_kernel,
+        name="transform",
+        out_shape=(
+            jax.ShapeDtypeStruct((2, 4, 96, N), F32),
+            jax.ShapeDtypeStruct((2, 48, 128), F32),
+        ),
+        in_specs=[vmem, vmem, vmem, vmem],
+        out_specs=(vmem, vmem),
+        scratch_shapes=[
+            pltpu.VMEM((N, 2 * N), F32),
             pltpu.VMEM((2 * N, 2 * N), BF16),
             pltpu.VMEM((2 * N, 2 * N), BF16),
-            pltpu.VMEM((N, 2 * N), F32),
             pltpu.VMEM((144, 2, 8, 128), F32),
             pltpu.VMEM((K, 2, 8, 128), F32),
             pltpu.VMEM((2, K, 8, 128), F32),
             pltpu.VMEM((144, 2, 8, 128), F32),
             pltpu.VMEM((2, 48, 128), F32),
-            pltpu.VMEM((2, 48, 128), F32),
-            dma((4,)), dma((4,)), dma((4,)), dma((4,)),
+            pltpu.SemaphoreType.REGULAR,
             dma, dma, dma, dma, dma, dma, dma, dma,
         ],
-        compiler_params=pltpu.CompilerParams(has_side_effects=True, vmem_limit_bytes=56 << 20),
-        cost_estimate=pl.CostEstimate(flops=10**10, bytes_accessed=10**7, transcendentals=0),
-    )(
-        fock, pot, chem_potential, spectral_bound,
-        impurity_orbitals.reshape(1, N), imp4, potential_of,
-        jnp.asarray(t_hi), jnp.asarray(t_lo),
-    )
+        compiler_params=pltpu.CompilerParams(
+            has_side_effects=True, collective_id=1, vmem_limit_bytes=48 << 20
+        ),
+    )(start, imp, jnp.asarray(t_hi), jnp.asarray(t_lo))
+    return pl.pallas_call(
+        store_kernel,
+        name="store",
+        out_shape=(
+            jax.ShapeDtypeStruct((2, 4, 96, N), F32),
+            jax.ShapeDtypeStruct((2, 2, 48, 48), F32),
+        ),
+        in_specs=[vmem, vmem],
+        out_specs=(anywhere, vmem),
+        scratch_shapes=[dma((2,))],
+    )(cells, f_in)
 
 
 def solution(mesh):

time: 121 us -> 114 us (0.942)
  Pallas kernels: 113 us -> 107 us
    pallas_call x1 -> x3, Pallas kernels: 113 us -> 107 us  [the longest x1 91.5 us: per_device(): pl.pallas_call(main_kernel, name='transform', out_shape=(jax.ShapeDtypeSt...]
    reshape x2 -> x1, local copies, waits for them, and re-layouts: 2.01 us -> 0.68 us  [per_device(): imp = impurity_orbitals.reshape(1, N)]
    unnamed x4 -> x14, local copies, waits for them, and re-layouts: 3.05 us -> 4.29 us
where the time goes in v1:
time: 114 us
  Pallas kernels  107 us (94%)
  local copies, waits for them, and re-layouts  4.97 us (4%)
  between operations  2.13 us (2%)
    pallas_call x1, Pallas kernels, per_device(): pl.pallas_call(main_kernel, name='transform', out_shape=(jax.ShapeDtypeSt...  91.5 us
    pallas_call x1, Pallas kernels, per_device(): pl.pallas_call(gather_kernel, name='gather', out_shape=jax.ShapeDtypeStru...  12.3 us
    unnamed x14, local copies, waits for them, and re-layouts  4.29 us
    pallas_call x1, Pallas kernels, per_device(): pl.pallas_call(store_kernel, name='store', out_shape=(jax.ShapeDtypeStruc...  2.94 us

profile of v1, /device:TPU:24, one launch (start us, length us, event | category | flops | bytes accessed | tf_op | source)
XLA Modules:
  0.0 113.8 jit_solution(6244724772363819797)
XLA Ops:
  1.9 0.7 reshape.11.imp
  2.6 0.0 copy-start
  2.6 1.3 %copy-done = f32[2,4,96,384]{3,2,1,0:T(8,128)S(1)} copy-done((f32[2,4,96,384]{3,2,1,0:T(8,128)S(1)}, f32[2,4,96,384]{3,2,1,0:T(8,128)}, u32[]{:S(2)}) %copy-start) | copy-done | bytes 1179672
  3.9 0.0 copy-start.5
  3.9 0.7 copy-done.5
  4.6 0.0 copy-start.6
  4.6 0.7 copy-done.6
  5.3 0.0 copy-start.2
  5.3 0.0 copy-start.3
  5.3 12.3 %gather.1.x_in = f32[384,768]{1,0:T(8,128)S(1)} custom-call(f32[2,4,96,384]{3,2,1,0:T(8,128)S(1)} %copy-done, f32[48,48]{1,0:T(8,128)S(1)} %bitcast.3, f32[1]{0:T(128)S(6)} %copy.10.chem, f32[1]{0:T(128)S(6)} %copy.11.bound, s32[1,384]{1,0:T(1,128)S(1)} %reshape.11.imp, s32[8]{0:T(128)S(1)} %copy-done.6), custom_call_target="tpu_custom_call" | custom-call | tf_op jit(solution)/shard_map/gather/pallas_call | solution.py:332
  17.6 0.0 copy-done.2
  17.6 0.0 copy-done.3
  17.6 91.5 %transform.1 = (f32[2,4,96,384]{3,2,1,0:T(8,128)S(1)}, f32[2,48,128]{2,1,0:T(8,128)S(1)}) custom-call(f32[384,768]{1,0:T(8,128)S(1)} %gather.1.x_in, s32[1,384]{1,0:T(1,128)S(1)} %reshape.11.imp, bf16[512,512]{1,0:T(8,128)(2,1)S(1)} %copy-done.3, bf16[512,512]{1,0:T(8,128)(2,1)S(1)} %copy-done.2), custom_call_target="tpu_custom_call" | custom-call | tf_op jit(solution)/shard_map/transform/pallas_call | solution.py:349
  109.1 0.0 copy-start.1
  109.1 1.0 copy-done.1
  110.1 0.0 copy-start.4
  110.1 0.6 copy-done.4
  110.7 2.9 %store.1 = (f32[2,4,96,384]{3,2,1,0:T(8,128)}, f32[2,2,48,48]{3,2,1,0:T(8,128)}) custom-call(f32[2,4,96,384]{3,2,1,0:T(8,128)} %copy-done.1, f32[2,48,128]{2,1,0:T(8,128)} %copy-done.4), custom_call_target="tpu_custom_call" | custom-call | tf_op jit(solution)/shard_map/store/pallas_call | solution.py:374
Async XLA Ops:
  2.6 1.3 %copy-start = (f32[2,4,96,384]{3,2,1,0:T(8,128)S(1)}, f32[2,4,96,384]{3,2,1,0:T(8,128)}, u32[]{:S(2)}) copy-start(f32[2,4,96,384]{3,2,1,0:T(8,128)} %fock.1) | copy-start | bytes 3538948
  3.9 0.7 copy-start.5
  4.6 0.7 copy-start.6
  5.3 12.3 %copy-start.2 = (bf16[512,512]{1,0:T(8,128)(2,1)S(1)}, bf16[512,512]{1,0:T(8,128)(2,1)}, u32[]{:S(2)}) copy-start(bf16[512,512]{1,0:T(8,128)(2,1)} %constant.5.clone.t_lo) | copy-start | bytes 1572868
  5.3 12.3 %copy-start.3 = (bf16[512,512]{1,0:T(8,128)(2,1)S(1)}, bf16[512,512]{1,0:T(8,128)(2,1)}, u32[]{:S(2)}) copy-start(bf16[512,512]{1,0:T(8,128)(2,1)} %constant.4.clone.t_hi) | copy-start | bytes 1572868
  109.1 1.0 copy-start.1
  110.1 0.6 copy-start.4

commit v2 on v1

--- a/solution.py
+++ b/solution.py
@@ -55,22 +55,35 @@
     return (3 - 3 * g) * (1 - yh) + (1 + g) * yh, ka - 36 * g
 
 
-def frag_device(o, rt):
-    far = (o % 3 == 0).astype(jnp.int32)
-    odd = o // 2
-    h = rt * 2 + odd
-    z = h % 8
-    return z * 8 + (z + 1 + 3 * (h // 8)) % 8, 2 * far
+def far_then_near(i):
+    odd = i % 2
+    return (1 - odd) * ((4 + i // 2) % 8) + odd * (3 - i // 2)
+
+
+def frag_device(g):
+    o = g % 4
+    return 8 * g + (g + 1) % 8, 2 - 2 * (((o + 1) // 2) % 2)
 
 
 def gather_kernel(
-    fock, pot, chem, bound, imp, pof, x_out, m_src, m_all, pot_all, u_ref, s_fock, r_fock, s_pot, r_pot
+    fock_hbm, pot_hbm, chem, bound, imp_hbm, pof_hbm, x_out,
+    fock, pot, imp_flat, pof, m_src, m_all, pot_all, u_ref, s_in, s_fock, r_fock, s_pot, r_pot,
 ):
     ka = lax.axis_index("ka")
     orb = lax.axis_index("orb")
     barrier = pltpu.get_barrier_semaphore()
     for step in (1, 2, 3):
         pl.semaphore_signal(barrier, inc=1, device_id=(ka, (orb + step) % 4), device_id_type=MESH)
+    loads = [
+        pltpu.make_async_copy(source, target, s_in.at[n])
+        for n, (source, target) in enumerate(
+            ((fock_hbm, fock), (pot_hbm, pot), (imp_hbm, imp_flat), (pof_hbm, pof))
+        )
+    ]
+    for load in loads:
+        load.start()
+    for load in loads:
+        load.wait()
     m_src[...] = fock[0] + fock[1]
     pl.semaphore_wait(barrier, 3)
     for step in (2, 3, 1):
@@ -97,7 +110,7 @@
     rows, cols = iota((N, N), 0), iota((N, N), 1)
     wide = jnp.where(rows // 48 == cols // 48, wide, 0.0)
     wide = 0.5 * (wide + wide.T)
-    place = (rows == imp[...]).astype(F32)
+    place = (rows == imp_flat[...].reshape(1, N)).astype(F32)
     u_ref[...] = contract(contract(place, wide, ((1,), (0,))), place, ((1,), (1,)))
 
     for step in (1, 2, 3):
@@ -116,9 +129,10 @@
 
 
 def main_kernel(
-    x_in, imp, t_hi, t_lo, cells, f_in,
+    x_in, imp_hbm, t_hi, t_lo, cells, f_in,
+    imp_flat,
     x_ref, w_hi, w_lo, d_tiles, k_buf, o_buf, d0_buf, f_out,
-    entered, s_k, r_k, s_o, r_o, s_d0, r_d0, s_f, r_f,
+    s_imp, entered, s_k, r_k, s_o, r_o, s_d0, r_d0, s_f, r_f,
 ):
     ka = lax.axis_index("ka")
     orb = lax.axis_index("orb")
@@ -132,6 +146,8 @@
         pl.semaphore_signal(barrier, inc=1, device_id=(8 * z + plane, (orb + d) % 4), device_id_type=MESH)
         return carry
 
+    fetch = pltpu.make_async_copy(imp_hbm, imp_flat, s_imp)
+    fetch.start()
     lax.fori_loop(1, 32, greet, 0)
     for step in range(1, 8):
         pl.semaphore_signal(barrier, inc=1, device_id=((ka + 8 * step) % 64, orb), device_id_type=MESH)
@@ -151,6 +167,7 @@
         c = dot3(s_hi, s_lo, w_hi[...], w_lo[...])
         x_ref[...] = 1.5 * x_ref[...] - 0.5 * c
         if step == 0:
+            fetch.wait()
             pl.semaphore_wait(barrier, 38)
             for hop in range(1, 8):
                 pl.semaphore_signal(entered, inc=1, device_id=((ka + 8 * hop) % 64, orb), device_id_type=MESH)
@@ -176,34 +193,36 @@
     def send_k(tile, to_ka, to_orb):
         remote(d_tiles.at[tile], k_buf.at[me], s_k, r_k, to_ka, to_orb).start()
 
-    def spread_k(d, carry):
-        to_z = (z + d % 8) % 8
-        to_x = (x + (d // 8) % 4) % 4
-        to_yl = (yl + (d // 32) % 2) % 2
-        to_yh = (yh + d // 64) % 2
-        to_ka = to_z * 8 + to_x * 2 + to_yl
-        o, j = tile_of(to_ka, to_yh)
-
-        @pl.when((d > 0) | (core == 0))
-        def _():
-            send_k(o * 36 + j, to_ka, to_yh * 2 + 1)
-
-        return carry
-
-    lax.fori_loop(0, 128, spread_k, 0)
-
-    def spread_extra(d, carry):
-        to_z = (z + d % 8) % 8
-        to_yh = (yh + d // 8) % 2
-        o = 2 - 2 * to_yh
-
-        @pl.when((d > 0) | jnp.logical_not(extra))
-        def _():
-            send_k(o * 36 + 28 + to_z, 9 * to_z, to_yh * 2)
-
-        return carry
-
-    lax.fori_loop(0, 16, spread_extra, 0)
+    for half in range(2):
+
+        def spread_k(d, carry, half=half):
+            step_z = far_then_near(d % 8)
+            to_z = (z + step_z) % 8
+            to_x = (x + (d // 8) % 4) % 4
+            to_yh = (yh + d // 32) % 2
+            to_ka = to_z * 8 + to_x * 2 + half
+            o, j = tile_of(to_ka, to_yh)
+
+            @pl.when((d != 7) | (yl != half) | (core == 0))
+            def _():
+                send_k(o * 36 + j, to_ka, to_yh * 2 + 1)
+
+            return carry
+
+        lax.fori_loop(0, 64, spread_k, 0)
+
+        def spread_extra(d, carry, half=half):
+            to_z = 2 * ((z // 2 + d % 4) % 4) + half
+            to_yh = (yh + d // 4) % 2
+            o = 2 - 2 * to_yh
+
+            @pl.when((d > 0) | (to_z != z) | jnp.logical_not(extra))
+            def _():
+                send_k(o * 36 + 28 + to_z, 9 * to_z, to_yh * 2)
+
+            return carry
+
+        lax.fori_loop(0, 8, spread_extra, 0)
 
     row, cb = t_j % 12, t_j // 12
 
@@ -226,14 +245,14 @@
                     o_rows[pl.ds(c * K * 8 + s, K, stride=8), :] = res[c * K : c * K + K, n * 128 : n * 128 + 128]
 
         def send_d0(g, carry):
-            to_ka, to_orb = frag_device(g % 4, g // 4)
+            to_ka, to_orb = frag_device(g)
             remote(o_buf.at[:, 0], d0_buf.at[t_o * 36 + t_j], s_d0, r_d0, to_ka, to_orb).start()
             return carry
 
-        lax.fori_loop(0, 24, send_d0, 0)
+        lax.fori_loop(0, 8, send_d0, 0)
 
         def send_o(d, carry):
-            to_z = (z + d % 8) % 8
+            to_z = (z + far_then_near(d % 8)) % 8
             to_x = (x + (d // 8) % 4) % 4
             to_yl = (yl + d // 32) % 2
             to_ka = to_z * 8 + to_x * 2 + to_yl
@@ -246,14 +265,12 @@
 
         lax.fori_loop(0, 64, send_o, 0)
 
-    turn = (ka % 8 + 8 - z) % 8
-    makes = (core == 0) & ((turn == 1) | ((turn == 4) & (z < 4)))
-    h = jnp.where(turn == 1, z, 8 + z)
-    f_rt, f_odd = h // 2, h % 2
-    f_o = jnp.where(yh == 1, 3 * f_odd, 1 + f_odd)
+    f_o, f_half = z % 4, z // 4
+    makes = (core == 0) & (ka % 8 == (z + 1) % 8) & (yh == 1 - ((f_o + 1) // 2) % 2)
 
     @pl.when(makes)
     def _():
+        imp = imp_flat[...].reshape(1, N)
         slots = [imp[:, 96 * o : 96 * o + 96] for o in range(4)]
         own_slots = slots[0]
         for o in range(1, 4):
@@ -274,8 +291,8 @@
             f_out[part] = jnp.where(left, picked[:48], picked[48:96])
 
         def send_f(d, carry):
-            to_ka = ((z + d % 8) % 8) * 8 + (ka + d // 8) % 8
-            rows_at = pl.ds(pl.multiple_of(8 * f_rt, 8), 8)
+            to_ka = ((z + far_then_near(d % 8)) % 8) * 8 + (ka + d // 8) % 8
+            rows_at = pl.ds(pl.multiple_of(24 * f_half, 8), 24)
             remote(f_out.at[:, rows_at], f_in.at[:, rows_at], s_f, r_f, to_ka, f_o).start()
             return carry
 
@@ -292,12 +309,12 @@
 
     @pl.when(has_tile)
     def _():
-        wait_bytes(d_tiles.at[pl.ds(0, 24)], s_d0)
+        wait_bytes(d_tiles.at[pl.ds(0, 8)], s_d0)
         wait_bytes(o_buf, s_o)
 
     @pl.when(makes)
     def _():
-        wait_bytes(d_tiles.at[pl.ds(0, 64)], s_f)
+        wait_bytes(k_buf.at[pl.ds(0, 192)], s_f)
 
 
 def store_kernel(cells, f_in, out, frag, sem):
@@ -325,27 +342,38 @@
     t_hi, t_lo = tables()
     vmem = pl.BlockSpec(memory_space=pltpu.VMEM)
     smem = pl.BlockSpec(memory_space=pltpu.SMEM)
-    anywhere = pl.BlockSpec(memory_space=pl.ANY)
+    hbm = pl.BlockSpec(memory_space=pltpu.HBM)
     dma = pltpu.SemaphoreType.DMA
     pot = potential.transpose(1, 0, 2).reshape(48, 48)
-    imp = impurity_orbitals.reshape(1, N)
+    imp = pltpu.with_memory_space_constraint(impurity_orbitals, pltpu.HBM)
     start = pl.pallas_call(
         gather_kernel,
         name="gather",
         out_shape=jax.ShapeDtypeStruct((N, 2 * N), F32),
-        in_specs=[vmem, vmem, smem, smem, vmem, smem],
+        in_specs=[hbm, hbm, smem, smem, hbm, hbm],
         out_specs=vmem,
         scratch_shapes=[
+            pltpu.VMEM((2, 4, 96, N), F32),
+            pltpu.VMEM((48, 48), F32),
+            pltpu.VMEM((N,), jnp.int32),
+            pltpu.SMEM((8,), jnp.int32),
             pltpu.VMEM((4, 96, N), F32),
             pltpu.VMEM((4, 96, N), F32),
             pltpu.VMEM((4, 48, 48), F32),
             pltpu.VMEM((N, N), F32),
-            dma((4,)), dma((4,)), dma((4,)), dma((4,)),
+            dma((4,)), dma((4,)), dma((4,)), dma((4,)), dma((4,)),
         ],
         compiler_params=pltpu.CompilerParams(
             has_side_effects=True, collective_id=0, vmem_limit_bytes=40 << 20
         ),
-    )(fock, pot, chem_potential, spectral_bound, imp, potential_of)
+    )(
+        pltpu.with_memory_space_constraint(fock, pltpu.HBM),
+        pltpu.with_memory_space_constraint(pot, pltpu.HBM),
+        chem_potential,
+        spectral_bound,
+        imp,
+        pltpu.with_memory_space_constraint(potential_of, pltpu.HBM),
+    )
     cells, f_in = pl.pallas_call(
         main_kernel,
         name="transform",
@@ -353,9 +381,10 @@
             jax.ShapeDtypeStruct((2, 4, 96, N), F32),
             jax.ShapeDtypeStruct((2, 48, 128), F32),
         ),
-        in_specs=[vmem, vmem, vmem, vmem],
+        in_specs=[vmem, hbm, vmem, vmem],
         out_specs=(vmem, vmem),
         scratch_shapes=[
+            pltpu.VMEM((N,), jnp.int32),
             pltpu.VMEM((N, 2 * N), F32),
             pltpu.VMEM((2 * N, 2 * N), BF16),
             pltpu.VMEM((2 * N, 2 * N), BF16),
@@ -364,6 +393,7 @@
             pltpu.VMEM((2, K, 8, 128), F32),
             pltpu.VMEM((144, 2, 8, 128), F32),
             pltpu.VMEM((2, 48, 128), F32),
+            dma,
             pltpu.SemaphoreType.REGULAR,
             dma, dma, dma, dma, dma, dma, dma, dma,
         ],
@@ -379,8 +409,9 @@
             jax.ShapeDtypeStruct((2, 2, 48, 48), F32),
         ),
         in_specs=[vmem, vmem],
-        out_specs=(anywhere, vmem),
+        out_specs=(hbm, vmem),
         scratch_shapes=[dma((2,))],
+        compiler_params=pltpu.CompilerParams(vmem_limit_bytes=4 << 20),
     )(cells, f_in)
 
 

time: 114 us -> 113 us (level)
  the two profiles are of different devices: /device:TPU:24 before, /device:TPU:1 now
where the time goes in v2:
time: 113 us; the launch traced here: 111 us
  Pallas kernels  109 us (96%)
  between operations  2.13 us (2%)
    pallas_call x1, Pallas kernels, per_device(): pl.pallas_call(main_kernel, name='transform', out_shape=(jax.ShapeDtypeSt...  92.4 us
    pallas_call x1, Pallas kernels, per_device(): pl.pallas_call(gather_kernel, name='gather', out_shape=jax.ShapeDtypeStru...  15 us

profile of v2, /device:TPU:1, one launch (start us, length us, event | category | flops | bytes accessed | tf_op | source)
XLA Modules:
  0.0 111.2 jit_solution(12832229227156549293)
XLA Ops:
  1.9 0.0 copy-start
  1.9 0.0 copy-start.1
  1.9 15.0 %gather.1.x_in = f32[384,768]{1,0:T(8,128)S(1)} custom-call(f32[2,4,96,384]{3,2,1,0:T(8,128)} %fock_hbm.1, f32[48,48]{1,0:T(8,128)} %bitcast.3, f32[1]{0:T(128)S(6)} %copy.10.chem, f32[1]{0:T(128)S(6)} %copy.11.bound, s32[384]{0:T(512)} %imp_hbm.3, s32[8]{0:T(128)} %pof_hbm.1), custom_call_target="tpu_custom_call" | custom-call | tf_op jit(solution)/shard_map/gather/pallas_call | solution.py:349
  16.9 0.0 copy-done
  17.0 0.0 copy-done.1
  17.0 92.4 %transform.1 = (f32[2,4,96,384]{3,2,1,0:T(8,128)S(1)}, f32[2,48,128]{2,1,0:T(8,128)S(1)}) custom-call(f32[384,768]{1,0:T(8,128)S(1)} %gather.1.x_in, s32[384]{0:T(512)} %imp_hbm.3, bf16[512,512]{1,0:T(8,128)(2,1)S(1)} %copy-done.1, bf16[512,512]{1,0:T(8,128)(2,1)S(1)} %copy-done), custom_call_target="tpu_custom_call" | custom-call | tf_op jit(solution)/shard_map/transform/pallas_call | solution.py:377
  109.4 1.7 %store.1 = (f32[2,4,96,384]{3,2,1,0:T(8,128)}, f32[2,2,48,48]{3,2,1,0:T(8,128)}) custom-call(f32[2,4,96,384]{3,2,1,0:T(8,128)S(1)} %get-tuple-element.4.cells, f32[2,48,128]{2,1,0:T(8,128)S(1)} %get-tuple-element.5.f_in), custom_call_target="tpu_custom_call" | custom-call | tf_op jit(solution)/shard_map/store/pallas_call | solution.py:404
Async XLA Ops:
  1.9 15.0 %copy-start = (bf16[512,512]{1,0:T(8,128)(2,1)S(1)}, bf16[512,512]{1,0:T(8,128)(2,1)}, u32[]{:S(2)}) copy-start(bf16[512,512]{1,0:T(8,128)(2,1)} %constant.5.clone.t_lo) | copy-start | bytes 1572868
  1.9 15.0 %copy-start.1 = (bf16[512,512]{1,0:T(8,128)(2,1)S(1)}, bf16[512,512]{1,0:T(8,128)(2,1)}, u32[]{:S(2)}) copy-start(bf16[512,512]{1,0:T(8,128)(2,1)} %constant.4.clone.t_hi) | copy-start | bytes 1572868

commit v3 on v2

--- a/solution.py
+++ b/solution.py
@@ -50,9 +50,49 @@
     pltpu.make_async_copy(ref, ref, sem).wait()
 
 
-def tile_of(ka, yh):
-    g = ka // 36
-    return (3 - 3 * g) * (1 - yh) + (1 + g) * yh, ka - 36 * g
+PAIRS = ((0, 1), (0, 2), (0, 3), (1, 2), (1, 3), (2, 3), (0, 0), (1, 1), (2, 2), (3, 3))
+TILES = 9 * len(PAIRS)
+
+
+def pack(block):
+    a, b, c, d = (block[24 * n : 24 * n + 24] for n in range(4))
+    return jnp.concatenate(
+        [
+            jnp.concatenate([a, b[:, :32]], axis=1),
+            jnp.concatenate([b[:, 32:], c[:, :64]], axis=1),
+            jnp.concatenate([c[:, 64:], d], axis=1),
+        ],
+        axis=0,
+    )
+
+
+def unpack(packed):
+    p, q, r = (packed[24 * n : 24 * n + 24] for n in range(3))
+    return jnp.concatenate(
+        [
+            p[:, :96],
+            jnp.concatenate([p[:, 96:], q[:, :64]], axis=1),
+            jnp.concatenate([q[:, 64:], r[:, :32]], axis=1),
+            r[:, 32:],
+        ],
+        axis=0,
+    )
+
+
+def blocks_of(pair):
+    late, last = (pair >= 3).astype(jnp.int32), (pair >= 5).astype(jnp.int32)
+    diagonal = pair >= 6
+    return (
+        jnp.where(diagonal, pair - 6, late + last),
+        jnp.where(diagonal, pair - 6, pair + 1 - 2 * late - last),
+    )
+
+
+def tile_at(z, x, yl, yh):
+    column = x * 4 + yh * 2 + yl
+    turn = (z + 16 - column) % 8
+    tile = (turn - turn // 4) * 16 + column
+    return tile, (turn % 4 != 3) & (tile < TILES)
 
 
 def far_then_near(i):
@@ -129,9 +169,9 @@
 
 
 def main_kernel(
-    x_in, imp_hbm, t_hi, t_lo, cells, f_in,
+    x_in, imp_hbm, t_hi, t_lo, landing, f_in,
     imp_flat,
-    x_ref, w_hi, w_lo, d_tiles, k_buf, o_buf, d0_buf, f_out,
+    x_ref, w_hi, w_lo, d_tiles, k_buf, o_buf, d0_buf, full, f_out,
     s_imp, entered, s_k, r_k, s_o, r_o, s_d0, r_d0, s_f, r_f,
 ):
     ka = lax.axis_index("ka")
@@ -171,82 +211,58 @@
             pl.semaphore_wait(barrier, 38)
             for hop in range(1, 8):
                 pl.semaphore_signal(entered, inc=1, device_id=((ka + 8 * hop) % 64, orb), device_id_type=MESH)
-    eye_half = 0.5 * eye
     for part in range(2):
-        for cb in range(3):
-            value = -0.5 * x_ref[:, part * N + cb * 128 : part * N + cb * 128 + 128]
-            if part == 0:
-                value = value + eye_half[:, cb * 128 : cb * 128 + 128]
-            value = value.reshape(4, 12, 8, 128)
-            for o in range(4):
-                base = o * 36 + cb * 12
-                d_tiles[base : base + 12, part] = value[o]
-
-    own_o, own_j = tile_of(ka, yh)
-    extra = (core == 0) & (ka == 9 * z)
-    has_tile = (core == 1) | extra
-    t_o = jnp.where(core == 1, own_o, jnp.where(yh == 1, 0, 2))
-    t_j = jnp.where(core == 1, own_j, 28 + z)
-
+        value = -0.5 * x_ref[:, part * N : part * N + N]
+        if part == 0:
+            value = value + 0.5 * eye
+        for n, (o, p) in enumerate(PAIRS):
+            packed = pack(value[96 * o : 96 * o + 96, 96 * p : 96 * p + 96])
+            d_tiles[9 * n : 9 * n + 9, part] = packed.reshape(9, 8, 128)
+
+    own_tile, chip_has = tile_at(z, x, yl, yh)
+    has_tile = (core == 1) & chip_has
     pl.semaphore_wait(entered, 7)
 
-    def send_k(tile, to_ka, to_orb):
-        remote(d_tiles.at[tile], k_buf.at[me], s_k, r_k, to_ka, to_orb).start()
-
-    for half in range(2):
-
-        def spread_k(d, carry, half=half):
-            step_z = far_then_near(d % 8)
-            to_z = (z + step_z) % 8
-            to_x = (x + (d // 8) % 4) % 4
-            to_yh = (yh + d // 32) % 2
-            to_ka = to_z * 8 + to_x * 2 + half
-            o, j = tile_of(to_ka, to_yh)
-
-            @pl.when((d != 7) | (yl != half) | (core == 0))
-            def _():
-                send_k(o * 36 + j, to_ka, to_yh * 2 + 1)
-
-            return carry
-
-        lax.fori_loop(0, 64, spread_k, 0)
-
-        def spread_extra(d, carry, half=half):
-            to_z = 2 * ((z // 2 + d % 4) % 4) + half
-            to_yh = (yh + d // 4) % 2
-            o = 2 - 2 * to_yh
-
-            @pl.when((d > 0) | (to_z != z) | jnp.logical_not(extra))
-            def _():
-                send_k(o * 36 + 28 + to_z, 9 * to_z, to_yh * 2)
-
-            return carry
-
-        lax.fori_loop(0, 8, spread_extra, 0)
-
-    row, cb = t_j % 12, t_j // 12
+    def spread_k(d, carry):
+        to_z = (z + far_then_near(d % 8)) % 8
+        to_x = (x + (d // 8) % 4) % 4
+        to_yl = (yl + (d // 32) % 2) % 2
+        to_yh = (yh + d // 64) % 2
+        tile, there = tile_at(to_z, to_x, to_yl, to_yh)
+
+        @pl.when(there & ((d != 7) | (core == 0)))
+        def _():
+            to_ka = to_z * 8 + to_x * 2 + to_yl
+            remote(d_tiles.at[tile], k_buf.at[me], s_k, r_k, to_ka, to_yh * 2 + 1).start()
+
+        return carry
+
+    lax.fori_loop(0, 128, spread_k, 0)
+    t_o, t_p = blocks_of(own_tile // 9)
+    t_m = own_tile % 9
+    mirrored = t_o != t_p
+    to_self = (t_o == orb) | (t_p == orb)
 
     @pl.when(has_tile)
     def _():
-        k_buf[me] = d_tiles[t_o * 36 + t_j]
+        k_buf[me] = d_tiles[own_tile]
         wait_bytes(k_buf.at[pl.ds(0, K - 1)], r_k)
         k_rows = k_buf.reshape(K * 16, 128)
-        o_rows = o_buf.reshape(2 * K * 8, 128)
-        for pair in range(4):
-            parts = []
-            for s in (2 * pair, 2 * pair + 1):
-                parts.append(
-                    jnp.concatenate([k_rows[pl.ds(c * 8 + s, K, stride=16), :] for c in range(2)], axis=0)
-                )
-            v_hi, v_lo = split2(jnp.concatenate(parts, axis=1))
+        o_rows = o_buf.reshape(4 * K * 8, 128)
+        for s in range(8):
+            both = [k_rows[pl.ds(c * 8 + s, K, stride=16), :] for c in range(2)]
+            v_hi, v_lo = split2(jnp.concatenate(both, axis=1))
             res = dot3(t_hi[...], t_lo[...], v_hi, v_lo)
-            for n, s in enumerate((2 * pair, 2 * pair + 1)):
-                for c in range(2):
-                    o_rows[pl.ds(c * K * 8 + s, K, stride=8), :] = res[c * K : c * K + K, n * 128 : n * 128 + 128]
+            cos_re, cos_im = res[:K, :128], res[:K, 128:]
+            sin_re, sin_im = res[K:, :128], res[K:, 128:]
+            o_rows[pl.ds(s, K, stride=8), :] = cos_re - sin_im
+            o_rows[pl.ds(K * 8 + s, K, stride=8), :] = cos_im + sin_re
+            o_rows[pl.ds(2 * K * 8 + s, K, stride=8), :] = cos_re + sin_im
+            o_rows[pl.ds(3 * K * 8 + s, K, stride=8), :] = sin_re - cos_im
 
         def send_d0(g, carry):
             to_ka, to_orb = frag_device(g)
-            remote(o_buf.at[:, 0], d0_buf.at[t_o * 36 + t_j], s_d0, r_d0, to_ka, to_orb).start()
+            remote(o_buf.at[pl.ds(0, 2), 0], d0_buf.at[own_tile], s_d0, r_d0, to_ka, to_orb).start()
             return carry
 
         lax.fori_loop(0, 8, send_d0, 0)
@@ -256,14 +272,27 @@
             to_x = (x + (d // 8) % 4) % 4
             to_yl = (yl + d // 32) % 2
             to_ka = to_z * 8 + to_x * 2 + to_yl
-            remote(
-                o_buf.at[:, pl.ds(4 * to_ka, 4)],
-                cells.at[:, :, pl.ds(pl.multiple_of(8 * row, 8), 8), pl.ds(pl.multiple_of(128 * cb, 128), 128)],
-                s_o, r_o, to_ka, t_o,
-            ).start()
+            cells_at = pl.ds(4 * to_ka, 4)
+
+            @pl.when((d != 7) | (t_o != orb))
+            def _():
+                remote(o_buf.at[pl.ds(0, 2), cells_at], landing.at[t_p * 9 + t_m], s_o, r_o, to_ka, t_o).start()
+
+            @pl.when(mirrored & ((d != 7) | (t_p != orb)))
+            def _():
+                remote(o_buf.at[pl.ds(2, 2), cells_at], landing.at[t_o * 9 + t_m], s_o, r_o, to_ka, t_p).start()
+
             return carry
 
         lax.fori_loop(0, 64, send_o, 0)
+
+        @pl.when(t_o == orb)
+        def _():
+            landing[t_p * 9 + t_m] = o_buf[:2, pl.ds(4 * ka, 4)]
+
+        @pl.when(mirrored & (t_p == orb))
+        def _():
+            landing[t_o * 9 + t_m] = o_buf[2:, pl.ds(4 * ka, 4)]
 
     f_o, f_half = z % 4, z // 4
     makes = (core == 0) & (ka % 8 == (z + 1) % 8) & (yh == 1 - ((f_o + 1) // 2) % 2)
@@ -280,14 +309,12 @@
         chosen = (iota((N, 128), 0) == own_slots).astype(F32)
         left = iota((48, 128), 1) < 48
         for part in range(2):
-            picked = jnp.zeros((128, 128), F32)
-            for cb in range(3):
-                block = jnp.concatenate(
-                    [d0_buf[o * 36 + cb * 12 : o * 36 + cb * 12 + 12, part].reshape(96, 128) for o in range(4)],
-                    axis=0,
-                )
-                some = contract(chosen, block, ((0,), (0,)))
-                picked = picked + contract(some, chosen[cb * 128 : cb * 128 + 128], ((1,), (0,)))
+            for n, (o, p) in enumerate(PAIRS):
+                block = unpack(d0_buf[9 * n : 9 * n + 9, part].reshape(72, 128))
+                full[96 * o : 96 * o + 96, 96 * p : 96 * p + 96] = block
+                if o != p:
+                    full[96 * p : 96 * p + 96, 96 * o : 96 * o + 96] = block.T if part == 0 else -block.T
+            picked = contract(contract(chosen, full[...], ((0,), (0,))), chosen, ((1,), (0,)))
             f_out[part] = jnp.where(left, picked[:48], picked[48:96])
 
         def send_f(d, carry):
@@ -299,28 +326,59 @@
         lax.fori_loop(0, 64, send_f, 0)
 
     wait_bytes(f_in, r_f)
-    wait_bytes(cells, r_o)
-
-    wait_bytes(d_tiles.at[pl.ds(0, 143)], s_k)
+    keeps = has_tile & to_self
+
+    @pl.when(keeps)
+    def _():
+        wait_bytes(landing.at[pl.ds(0, 35)], r_o)
+
+    @pl.when(jnp.logical_not(keeps))
+    def _():
+        wait_bytes(landing, r_o)
+
+    @pl.when(has_tile)
+    def _():
+        wait_bytes(d_tiles.at[pl.ds(0, TILES - 1)], s_k)
+        wait_bytes(d_tiles.at[pl.ds(0, 8)], s_d0)
 
     @pl.when(jnp.logical_not(has_tile))
     def _():
-        wait_bytes(d_tiles.at[0], s_k)
-
-    @pl.when(has_tile)
-    def _():
-        wait_bytes(d_tiles.at[pl.ds(0, 8)], s_d0)
-        wait_bytes(o_buf, s_o)
+        wait_bytes(d_tiles, s_k)
+
+    sides = ((mirrored, o_buf, K - 2), (jnp.logical_not(mirrored), o_buf.at[pl.ds(0, 2)], K - 4))
+    for side, sent, fewer in sides:
+
+        @pl.when(has_tile & side & to_self)
+        def _(sent=sent, fewer=fewer):
+            wait_bytes(sent.at[:, pl.ds(0, fewer)], s_o)
+
+        @pl.when(has_tile & side & jnp.logical_not(to_self))
+        def _(sent=sent):
+            wait_bytes(sent, s_o)
 
     @pl.when(makes)
     def _():
         wait_bytes(k_buf.at[pl.ds(0, 192)], s_f)
 
 
-def store_kernel(cells, f_in, out, frag, sem):
-    stores = [pltpu.make_async_copy(cells.at[c], out.at[c], sem.at[c]) for c in range(2)]
-    for store in stores:
-        store.start()
+def store_kernel(landing, f_in, out, frag, buf, sem):
+    own = lax.axis_index("orb")
+    stores = []
+    for c in range(2):
+        for r in range(4):
+            for q in range(4):
+                block = unpack(landing[9 * q : 9 * q + 9, c, r].reshape(72, 128))
+
+                @pl.when(own <= q)
+                def _(block=block, c=c, r=r, q=q):
+                    buf[c, r, :, 96 * q : 96 * q + 96] = block
+
+                @pl.when(own > q)
+                def _(block=block, c=c, r=r, q=q):
+                    buf[c, r, :, 96 * q : 96 * q + 96] = block.T
+
+            stores.append(pltpu.make_async_copy(buf.at[c, r], out.at[c, r], sem.at[c, r]))
+            stores[-1].start()
     for part in range(2):
         for f in range(2):
             frag[part, f] = f_in[part, :, 48 * f : 48 * f + 48]
@@ -332,7 +390,7 @@
     grid = np.outer(np.arange(K), np.arange(K)) % K
     angle = grid * (2.0 * math.pi / K)
     c, s = np.cos(angle) / K, np.sin(angle) / K
-    full = np.block([[c, -s], [s, c]]).astype(np.float32)
+    full = np.concatenate([c, s]).astype(np.float32)
     hi = full.astype(jnp.bfloat16)
     lo = (full - hi.astype(np.float32)).astype(jnp.bfloat16)
     return hi, lo
@@ -374,11 +432,11 @@
         imp,
         pltpu.with_memory_space_constraint(potential_of, pltpu.HBM),
     )
-    cells, f_in = pl.pallas_call(
+    landing, f_in = pl.pallas_call(
         main_kernel,
         name="transform",
         out_shape=(
-            jax.ShapeDtypeStruct((2, 4, 96, N), F32),
+            jax.ShapeDtypeStruct((36, 2, 4, 8, 128), F32),
             jax.ShapeDtypeStruct((2, 48, 128), F32),
         ),
         in_specs=[vmem, hbm, vmem, vmem],
@@ -388,10 +446,11 @@
             pltpu.VMEM((N, 2 * N), F32),
             pltpu.VMEM((2 * N, 2 * N), BF16),
             pltpu.VMEM((2 * N, 2 * N), BF16),
-            pltpu.VMEM((144, 2, 8, 128), F32),
+            pltpu.VMEM((TILES, 2, 8, 128), F32),
             pltpu.VMEM((K, 2, 8, 128), F32),
-            pltpu.VMEM((2, K, 8, 128), F32),
-            pltpu.VMEM((144, 2, 8, 128), F32),
+            pltpu.VMEM((4, K, 8, 128), F32),
+            pltpu.VMEM((TILES, 2, 8, 128), F32),
+            pltpu.VMEM((N, N), F32),
             pltpu.VMEM((2, 48, 128), F32),
             dma,
             pltpu.SemaphoreType.REGULAR,
@@ -410,9 +469,9 @@
         ),
         in_specs=[vmem, vmem],
         out_specs=(hbm, vmem),
-        scratch_shapes=[dma((2,))],
-        compiler_params=pltpu.CompilerParams(vmem_limit_bytes=4 << 20),
-    )(cells, f_in)
+        scratch_shapes=[pltpu.VMEM((2, 4, 96, N), F32), dma((2, 4))],
+        compiler_params=pltpu.CompilerParams(vmem_limit_bytes=8 << 20),
+    )(landing, f_in)
 
 
 def solution(mesh):

time: 113 us -> 115 us (1.018)
  the two profiles are of different devices: /device:TPU:1 before, /device:TPU:29 now
where the time goes in v3:
time: 115 us
  Pallas kernels  113 us (98%)
  between operations  2.13 us (2%)
    pallas_call x1, Pallas kernels, per_device(): pl.pallas_call(main_kernel, name='transform', out_shape=(jax.ShapeDtypeSt...  93 us
    pallas_call x1, Pallas kernels, per_device(): pl.pallas_call(gather_kernel, name='gather', out_shape=jax.ShapeDtypeStru...  12.5 us
    pallas_call x1, Pallas kernels, per_device(): pl.pallas_call(store_kernel, name='store', out_shape=(jax.ShapeDtypeStruc...  7.38 us

profile of v3, /device:TPU:29, one launch (start us, length us, event | category | flops | bytes accessed | tf_op | source)
XLA Modules:
  0.0 115.0 jit_solution(3549828952288550832)
XLA Ops:
  1.9 0.0 copy-start
  1.9 0.0 copy-start.1
  1.9 12.5 %gather.1.x_in = f32[384,768]{1,0:T(8,128)S(1)} custom-call(f32[2,4,96,384]{3,2,1,0:T(8,128)} %fock_hbm.1, f32[48,48]{1,0:T(8,128)} %bitcast.3, f32[1]{0:T(128)S(6)} %copy.10.chem, f32[1]{0:T(128)S(6)} %copy.11.bound, s32[384]{0:T(512)} %imp_hbm.3, s32[8]{0:T(128)} %pof_hbm.1), custom_call_target="tpu_custom_call" | custom-call | tf_op jit(solution)/shard_map/gather/pallas_call | solution.py:407
  14.4 0.0 copy-done
  14.4 0.0 copy-done.1
  14.4 93.0 %transform.1 = (f32[36,2,4,8,128]{4,3,2,1,0:T(8,128)S(1)}, f32[2,48,128]{2,1,0:T(8,128)S(1)}) custom-call(f32[384,768]{1,0:T(8,128)S(1)} %gather.1.x_in, s32[384]{0:T(512)} %imp_hbm.3, bf16[512,256]{1,0:T(8,128)(2,1)S(1)} %copy-done.1, bf16[512,256]{1,0:T(8,128)(2,1)S(1)} %copy-done), custom_call_target="tpu_custom_call" | custom-call | tf_op jit(solution)/shard_map/transform/pallas_call | solution.py:435
  107.5 7.4 %store.1 = (f32[2,4,96,384]{3,2,1,0:T(8,128)}, f32[2,2,48,48]{3,2,1,0:T(8,128)}) custom-call(f32[36,2,4,8,128]{4,3,2,1,0:T(8,128)S(1)} %get-tuple-element.4.landing, f32[2,48,128]{2,1,0:T(8,128)S(1)} %get-tuple-element.5.f_in), custom_call_target="tpu_custom_call" | custom-call | tf_op jit(solution)/shard_map/store/pallas_call | solution.py:463
Async XLA Ops:
  1.9 12.5 %copy-start = (bf16[512,256]{1,0:T(8,128)(2,1)S(1)}, bf16[512,256]{1,0:T(8,128)(2,1)}, u32[]{:S(2)}) copy-start(bf16[512,256]{1,0:T(8,128)(2,1)} %constant.5.clone.t_lo) | copy-start | bytes 786436
  1.9 12.5 %copy-start.1 = (bf16[512,256]{1,0:T(8,128)(2,1)S(1)}, bf16[512,256]{1,0:T(8,128)(2,1)}, u32[]{:S(2)}) copy-start(bf16[512,256]{1,0:T(8,128)(2,1)} %constant.4.clone.t_hi) | copy-start | bytes 786436

commit v4 on v3

--- a/solution.py
+++ b/solution.py
@@ -51,7 +51,7 @@
 
 
 PAIRS = ((0, 1), (0, 2), (0, 3), (1, 2), (1, 3), (2, 3), (0, 0), (1, 1), (2, 2), (3, 3))
-TILES = 9 * len(PAIRS)
+TILES = 18 * len(PAIRS)
 
 
 def pack(block):
@@ -88,11 +88,16 @@
     )
 
 
-def tile_at(z, x, yl, yh):
-    column = x * 4 + yh * 2 + yl
+def column_of(x, yl, yh):
+    return x * 4 + yh * 2 + yl
+
+
+def tiles_at(z, column):
     turn = (z + 16 - column) % 8
-    tile = (turn - turn // 4) * 16 + column
-    return tile, (turn % 4 != 3) & (tile < TILES)
+    late = (turn == 6) & (column >= 12)
+    first = jnp.where(turn == 7, 124 + column, jnp.where(late, 164 + column, turn * 16 + column))
+    second = jnp.where(turn == 7, 108, jnp.where(turn == 1, 140, jnp.where(turn == 5, 156, 160))) + column
+    return first, second, (turn == 7) | (turn == 1) | (turn == 5) | late
 
 
 def far_then_near(i):
@@ -101,8 +106,8 @@
 
 
 def frag_device(g):
-    o = g % 4
-    return 8 * g + (g + 1) % 8, 2 - 2 * (((o + 1) // 2) % 2)
+    column = (g + 6) % 8
+    return 8 * g + 2 * (column // 4) + column % 2, 2 * ((column // 2) % 2)
 
 
 def gather_kernel(
@@ -211,16 +216,19 @@
             pl.semaphore_wait(barrier, 38)
             for hop in range(1, 8):
                 pl.semaphore_signal(entered, inc=1, device_id=((ka + 8 * hop) % 64, orb), device_id_type=MESH)
-    for part in range(2):
-        value = -0.5 * x_ref[:, part * N : part * N + N]
-        if part == 0:
-            value = value + 0.5 * eye
-        for n, (o, p) in enumerate(PAIRS):
-            packed = pack(value[96 * o : 96 * o + 96, 96 * p : 96 * p + 96])
-            d_tiles[9 * n : 9 * n + 9, part] = packed.reshape(9, 8, 128)
-
-    own_tile, chip_has = tile_at(z, x, yl, yh)
-    has_tile = (core == 1) & chip_has
+    values = (0.5 * eye - 0.5 * x_ref[:, :N], -0.5 * x_ref[:, N:])
+    for n, (o, p) in enumerate(PAIRS):
+        re, im = (pack(v[96 * o : 96 * o + 96, 96 * p : 96 * p + 96]).reshape(9, 8, 128) for v in values)
+        for half in range(2):
+            rows_at = slice(4 * half, 4 * half + 4)
+            d_tiles[18 * n + 9 * half : 18 * n + 9 * half + 9] = jnp.concatenate(
+                [re[:, rows_at], im[:, rows_at]], axis=1
+            )
+
+    column = column_of(x, yl, yh)
+    first, second, has_second = tiles_at(z, column)
+    own_tile = jnp.where(core == 1, first, second)
+    has_tile = (core == 1) | has_second
     pl.semaphore_wait(entered, 7)
 
     def spread_k(d, carry):
@@ -228,18 +236,22 @@
         to_x = (x + (d // 8) % 4) % 4
         to_yl = (yl + (d // 32) % 2) % 2
         to_yh = (yh + d // 64) % 2
-        tile, there = tile_at(to_z, to_x, to_yl, to_yh)
-
-        @pl.when(there & ((d != 7) | (core == 0)))
+        to_first, to_second, there = tiles_at(to_z, column_of(to_x, to_yl, to_yh))
+        to_ka = to_z * 8 + to_x * 2 + to_yl
+
+        @pl.when((d != 7) | (core == 0))
         def _():
-            to_ka = to_z * 8 + to_x * 2 + to_yl
-            remote(d_tiles.at[tile], k_buf.at[me], s_k, r_k, to_ka, to_yh * 2 + 1).start()
+            remote(d_tiles.at[to_first], k_buf.at[me], s_k, r_k, to_ka, to_yh * 2 + 1).start()
+
+        @pl.when(there & ((d != 7) | (core == 1)))
+        def _():
+            remote(d_tiles.at[to_second], k_buf.at[me], s_k, r_k, to_ka, to_yh * 2).start()
 
         return carry
 
     lax.fori_loop(0, 128, spread_k, 0)
-    t_o, t_p = blocks_of(own_tile // 9)
-    t_m = own_tile % 9
+    t_o, t_p = blocks_of(own_tile // 18)
+    t_m = own_tile % 18
     mirrored = t_o != t_p
     to_self = (t_o == orb) | (t_p == orb)
 
@@ -247,22 +259,22 @@
     def _():
         k_buf[me] = d_tiles[own_tile]
         wait_bytes(k_buf.at[pl.ds(0, K - 1)], r_k)
-        k_rows = k_buf.reshape(K * 16, 128)
-        o_rows = o_buf.reshape(4 * K * 8, 128)
-        for s in range(8):
-            both = [k_rows[pl.ds(c * 8 + s, K, stride=16), :] for c in range(2)]
+        k_rows = k_buf.reshape(K * 8, 128)
+        o_rows = o_buf.reshape(2 * K * 8, 128)
+        for s in range(4):
+            both = [k_rows[pl.ds(c * 4 + s, K, stride=8), :] for c in range(2)]
             v_hi, v_lo = split2(jnp.concatenate(both, axis=1))
             res = dot3(t_hi[...], t_lo[...], v_hi, v_lo)
             cos_re, cos_im = res[:K, :128], res[:K, 128:]
             sin_re, sin_im = res[K:, :128], res[K:, 128:]
             o_rows[pl.ds(s, K, stride=8), :] = cos_re - sin_im
-            o_rows[pl.ds(K * 8 + s, K, stride=8), :] = cos_im + sin_re
-            o_rows[pl.ds(2 * K * 8 + s, K, stride=8), :] = cos_re + sin_im
-            o_rows[pl.ds(3 * K * 8 + s, K, stride=8), :] = sin_re - cos_im
+            o_rows[pl.ds(4 + s, K, stride=8), :] = cos_im + sin_re
+            o_rows[pl.ds(K * 8 + s, K, stride=8), :] = cos_re + sin_im
+            o_rows[pl.ds(K * 8 + 4 + s, K, stride=8), :] = sin_re - cos_im
 
         def send_d0(g, carry):
             to_ka, to_orb = frag_device(g)
-            remote(o_buf.at[pl.ds(0, 2), 0], d0_buf.at[own_tile], s_d0, r_d0, to_ka, to_orb).start()
+            remote(o_buf.at[0, 0], d0_buf.at[own_tile], s_d0, r_d0, to_ka, to_orb).start()
             return carry
 
         lax.fori_loop(0, 8, send_d0, 0)
@@ -276,11 +288,11 @@
 
             @pl.when((d != 7) | (t_o != orb))
             def _():
-                remote(o_buf.at[pl.ds(0, 2), cells_at], landing.at[t_p * 9 + t_m], s_o, r_o, to_ka, t_o).start()
+                remote(o_buf.at[0, cells_at], landing.at[t_p * 18 + t_m], s_o, r_o, to_ka, t_o).start()
 
             @pl.when(mirrored & ((d != 7) | (t_p != orb)))
             def _():
-                remote(o_buf.at[pl.ds(2, 2), cells_at], landing.at[t_o * 9 + t_m], s_o, r_o, to_ka, t_p).start()
+                remote(o_buf.at[1, cells_at], landing.at[t_o * 18 + t_m], s_o, r_o, to_ka, t_p).start()
 
             return carry
 
@@ -288,14 +300,14 @@
 
         @pl.when(t_o == orb)
         def _():
-            landing[t_p * 9 + t_m] = o_buf[:2, pl.ds(4 * ka, 4)]
+            landing[t_p * 18 + t_m] = o_buf[0, pl.ds(4 * ka, 4)]
 
         @pl.when(mirrored & (t_p == orb))
         def _():
-            landing[t_o * 9 + t_m] = o_buf[2:, pl.ds(4 * ka, 4)]
+            landing[t_o * 18 + t_m] = o_buf[1, pl.ds(4 * ka, 4)]
 
     f_o, f_half = z % 4, z // 4
-    makes = (core == 0) & (ka % 8 == (z + 1) % 8) & (yh == 1 - ((f_o + 1) // 2) % 2)
+    makes = (core == 0) & (column == (z + 6) % 8)
 
     @pl.when(makes)
     def _():
@@ -310,7 +322,8 @@
         left = iota((48, 128), 1) < 48
         for part in range(2):
             for n, (o, p) in enumerate(PAIRS):
-                block = unpack(d0_buf[9 * n : 9 * n + 9, part].reshape(72, 128))
+                halves = [d0_buf[18 * n + 9 * h : 18 * n + 9 * h + 9, 4 * part : 4 * part + 4] for h in range(2)]
+                block = unpack(jnp.concatenate(halves, axis=1).reshape(72, 128))
                 full[96 * o : 96 * o + 96, 96 * p : 96 * p + 96] = block
                 if o != p:
                     full[96 * p : 96 * p + 96, 96 * o : 96 * o + 96] = block.T if part == 0 else -block.T
@@ -330,7 +343,7 @@
 
     @pl.when(keeps)
     def _():
-        wait_bytes(landing.at[pl.ds(0, 35)], r_o)
+        wait_bytes(landing.at[pl.ds(0, 71)], r_o)
 
     @pl.when(jnp.logical_not(keeps))
     def _():
@@ -345,12 +358,14 @@
     def _():
         wait_bytes(d_tiles, s_k)
 
-    sides = ((mirrored, o_buf, K - 2), (jnp.logical_not(mirrored), o_buf.at[pl.ds(0, 2)], K - 4))
-    for side, sent, fewer in sides:
+    for side, sent, fewer in (
+        (mirrored, o_buf, o_buf.at[:, pl.ds(0, K - 2)]),
+        (jnp.logical_not(mirrored), o_buf.at[0], o_buf.at[0, pl.ds(0, K - 4)]),
+    ):
 
         @pl.when(has_tile & side & to_self)
-        def _(sent=sent, fewer=fewer):
-            wait_bytes(sent.at[:, pl.ds(0, fewer)], s_o)
+        def _(fewer=fewer):
+            wait_bytes(fewer, s_o)
 
         @pl.when(has_tile & side & jnp.logical_not(to_self))
         def _(sent=sent):
@@ -358,31 +373,34 @@
 
     @pl.when(makes)
     def _():
-        wait_bytes(k_buf.at[pl.ds(0, 192)], s_f)
+        wait_bytes(o_buf.at[:, pl.ds(0, 192)], s_f)
 
 
 def store_kernel(landing, f_in, out, frag, buf, sem):
     own = lax.axis_index("orb")
-    stores = []
-    for c in range(2):
-        for r in range(4):
-            for q in range(4):
-                block = unpack(landing[9 * q : 9 * q + 9, c, r].reshape(72, 128))
-
-                @pl.when(own <= q)
-                def _(block=block, c=c, r=r, q=q):
-                    buf[c, r, :, 96 * q : 96 * q + 96] = block
-
-                @pl.when(own > q)
-                def _(block=block, c=c, r=r, q=q):
-                    buf[c, r, :, 96 * q : 96 * q + 96] = block.T
-
-            stores.append(pltpu.make_async_copy(buf.at[c, r], out.at[c, r], sem.at[c, r]))
-            stores[-1].start()
+    stores = [
+        [pltpu.make_async_copy(buf.at[c, r], out.at[c, r], sem.at[c, r]) for r in range(4)] for c in range(2)
+    ]
+    for place in range(4):
+
+        @pl.when(own == place)
+        def _(place=place):
+            for r in range(4):
+                for c in range(2):
+                    blocks = []
+                    for q in range(4):
+                        halves = [
+                            landing[18 * q + 9 * h : 18 * q + 9 * h + 9, r, 4 * c : 4 * c + 4] for h in range(2)
+                        ]
+                        block = unpack(jnp.concatenate(halves, axis=1).reshape(72, 128))
+                        blocks.append(block if place <= q else block.T)
+                    buf[c, r] = jnp.concatenate(blocks, axis=1)
+                    stores[c][r].start()
+
     for part in range(2):
         for f in range(2):
             frag[part, f] = f_in[part, :, 48 * f : 48 * f + 48]
-    for store in stores:
+    for store in stores[0] + stores[1]:
         store.wait()
 
 
@@ -436,7 +454,7 @@
         main_kernel,
         name="transform",
         out_shape=(
-            jax.ShapeDtypeStruct((36, 2, 4, 8, 128), F32),
+            jax.ShapeDtypeStruct((72, 4, 8, 128), F32),
             jax.ShapeDtypeStruct((2, 48, 128), F32),
         ),
         in_specs=[vmem, hbm, vmem, vmem],
@@ -446,10 +464,10 @@
             pltpu.VMEM((N, 2 * N), F32),
             pltpu.VMEM((2 * N, 2 * N), BF16),
             pltpu.VMEM((2 * N, 2 * N), BF16),
-            pltpu.VMEM((TILES, 2, 8, 128), F32),
-            pltpu.VMEM((K, 2, 8, 128), F32),
-            pltpu.VMEM((4, K, 8, 128), F32),
-            pltpu.VMEM((TILES, 2, 8, 128), F32),
+            pltpu.VMEM((TILES, 8, 128), F32),
+            pltpu.VMEM((K, 8, 128), F32),
+            pltpu.VMEM((2, K, 8, 128), F32),
+            pltpu.VMEM((TILES, 8, 128), F32),
             pltpu.VMEM((N, N), F32),
             pltpu.VMEM((2, 48, 128), F32),
             dma,

time: 115 us -> 95.1 us (0.83)
  the two profiles are of different devices: /device:TPU:29 before, /device:TPU:1 now
where the time goes in v4:
time: 95.1 us; the launch traced here: 95 us
  Pallas kernels  92.8 us (98%)
  between operations  2.13 us (2%)
    pallas_call x1, Pallas kernels, per_device(): pl.pallas_call(main_kernel, name='transform', out_shape=(jax.ShapeDtypeSt...  74.8 us
    pallas_call x1, Pallas kernels, per_device(): pl.pallas_call(gather_kernel, name='gather', out_shape=jax.ShapeDtypeStru...  15 us
    pallas_call x1, Pallas kernels, per_device(): pl.pallas_call(store_kernel, name='store', out_shape=(jax.ShapeDtypeStruc...  3.02 us

profile of v4, /device:TPU:1, one launch (start us, length us, event | category | flops | bytes accessed | tf_op | source)
XLA Modules:
  0.0 95.0 jit_solution(6959939781200180835)
XLA Ops:
  1.9 0.0 copy-start
  1.9 0.0 copy-start.1
  1.9 15.0 %gather.1.x_in = f32[384,768]{1,0:T(8,128)S(1)} custom-call(f32[2,4,96,384]{3,2,1,0:T(8,128)} %fock_hbm.1, f32[48,48]{1,0:T(8,128)} %bitcast.3, f32[1]{0:T(128)S(6)} %copy.10.chem, f32[1]{0:T(128)S(6)} %copy.11.bound, s32[384]{0:T(512)} %imp_hbm.3, s32[8]{0:T(128)} %pof_hbm.1), custom_call_target="tpu_custom_call" | custom-call | tf_op jit(solution)/shard_map/gather/pallas_call | solution.py:425
  16.9 0.0 copy-done
  17.0 0.0 copy-done.1
  17.0 74.8 %transform.1 = (f32[72,4,8,128]{3,2,1,0:T(8,128)S(1)}, f32[2,48,128]{2,1,0:T(8,128)S(1)}) custom-call(f32[384,768]{1,0:T(8,128)S(1)} %gather.1.x_in, s32[384]{0:T(512)} %imp_hbm.3, bf16[512,256]{1,0:T(8,128)(2,1)S(1)} %copy-done.1, bf16[512,256]{1,0:T(8,128)(2,1)S(1)} %copy-done), custom_call_target="tpu_custom_call" | custom-call | tf_op jit(solution)/shard_map/transform/pallas_call | solution.py:453
  91.8 3.0 %store.1 = (f32[2,4,96,384]{3,2,1,0:T(8,128)}, f32[2,2,48,48]{3,2,1,0:T(8,128)}) custom-call(f32[72,4,8,128]{3,2,1,0:T(8,128)S(1)} %get-tuple-element.4.landing, f32[2,48,128]{2,1,0:T(8,128)S(1)} %get-tuple-element.5.f_in), custom_call_target="tpu_custom_call" | custom-call | tf_op jit(solution)/shard_map/store/pallas_call | solution.py:481
Async XLA Ops:
  1.9 15.0 %copy-start = (bf16[512,256]{1,0:T(8,128)(2,1)S(1)}, bf16[512,256]{1,0:T(8,128)(2,1)}, u32[]{:S(2)}) copy-start(bf16[512,256]{1,0:T(8,128)(2,1)} %constant.5.clone.t_lo) | copy-start | bytes 786436
  1.9 15.0 %copy-start.1 = (bf16[512,256]{1,0:T(8,128)(2,1)S(1)}, bf16[512,256]{1,0:T(8,128)(2,1)}, u32[]{:S(2)}) copy-start(bf16[512,256]{1,0:T(8,128)(2,1)} %constant.4.clone.t_hi) | copy-start | bytes 786436

commit v5 on v4

--- a/solution.py
+++ b/solution.py
@@ -88,21 +88,32 @@
     )
 
 
-def column_of(x, yl, yh):
-    return x * 4 + yh * 2 + yl
-
-
-def tiles_at(z, column):
-    turn = (z + 16 - column) % 8
+def slots():
+    at = {}
+    for column in range(16):
+        for turn in range(8):
+            tile = turn * 16 + column
+            if turn == 7:
+                tile = 124 + column
+            elif turn == 6 and column >= 12:
+                tile = 164 + column
+            at[tile] = turn * 16 + column
+        for n, first in enumerate((108, 140, 156)):
+            at[first + column] = 128 + 16 * n + column
+        if column >= 12:
+            at[160 + column] = 164 + column
+    return at
+
+
+def own_tiles(turn, column):
     late = (turn == 6) & (column >= 12)
     first = jnp.where(turn == 7, 124 + column, jnp.where(late, 164 + column, turn * 16 + column))
     second = jnp.where(turn == 7, 108, jnp.where(turn == 1, 140, jnp.where(turn == 5, 156, 160))) + column
-    return first, second, (turn == 7) | (turn == 1) | (turn == 5) | late
-
-
-def far_then_near(i):
-    odd = i % 2
-    return (1 - odd) * ((4 + i // 2) % 8) + odd * (3 - i // 2)
+    slot = jnp.where(turn == 7, 128, jnp.where(turn == 1, 144, jnp.where(turn == 5, 160, 164))) + column
+    return first, turn * 16 + column, second, slot, (turn == 7) | (turn == 1) | (turn == 5) | late
+
+
+STEPS = (4, 3, 5, 2, 6, 1, 7, 0)
 
 
 def frag_device(g):
@@ -216,40 +227,75 @@
             pl.semaphore_wait(barrier, 38)
             for hop in range(1, 8):
                 pl.semaphore_signal(entered, inc=1, device_id=((ka + 8 * hop) % 64, orb), device_id_type=MESH)
+    slot_of_tile = slots()
     values = (0.5 * eye - 0.5 * x_ref[:, :N], -0.5 * x_ref[:, N:])
     for n, (o, p) in enumerate(PAIRS):
         re, im = (pack(v[96 * o : 96 * o + 96, 96 * p : 96 * p + 96]).reshape(9, 8, 128) for v in values)
         for half in range(2):
             rows_at = slice(4 * half, 4 * half + 4)
-            d_tiles[18 * n + 9 * half : 18 * n + 9 * half + 9] = jnp.concatenate(
-                [re[:, rows_at], im[:, rows_at]], axis=1
-            )
-
-    column = column_of(x, yl, yh)
-    first, second, has_second = tiles_at(z, column)
+            quads = jnp.concatenate([re[:, rows_at], im[:, rows_at]], axis=1)
+            for t in range(9):
+                d_tiles[slot_of_tile[18 * n + 9 * half + t]] = quads[t]
+
+    column = x * 4 + yh * 2 + yl
+    turn = lax.rem(z + 16 - column, 8)
+    first, first_slot, second, second_slot, has_second = own_tiles(turn, column)
     own_tile = jnp.where(core == 1, first, second)
+    own_slot = jnp.where(core == 1, first_slot, second_slot)
     has_tile = (core == 1) | has_second
     pl.semaphore_wait(entered, 7)
 
-    def spread_k(d, carry):
-        to_z = (z + far_then_near(d % 8)) % 8
-        to_x = (x + (d // 8) % 4) % 4
-        to_yl = (yl + (d // 32) % 2) % 2
-        to_yh = (yh + d // 64) % 2
-        to_first, to_second, there = tiles_at(to_z, column_of(to_x, to_yl, to_yh))
-        to_ka = to_z * 8 + to_x * 2 + to_yl
-
-        @pl.when((d != 7) | (core == 0))
+    def send_k(slot, to_ka, to_orb):
+        remote(d_tiles.at[slot], k_buf.at[me], s_k, r_k, to_ka, to_orb).start()
+
+    def column_at(e):
+        to_x = lax.rem(x + lax.rem(e, 4), 4)
+        to_yl = lax.rem(yl + lax.rem(lax.div(e, 4), 2), 2)
+        to_yh = lax.rem(yh + lax.div(e, 8), 2)
+        return to_x * 4 + to_yh * 2 + to_yl, to_x * 2 + to_yl, to_yh * 2
+
+    def spread_first(e, carry):
+        to_column, to_line, to_orb = column_at(e)
+        for step in STEPS:
+            to_z = lax.rem(z + step, 8)
+            slot = lax.rem(to_z + 16 - to_column, 8) * 16 + to_column
+            if step:
+                send_k(slot, to_z * 8 + to_line, to_orb + 1)
+            else:
+
+                @pl.when((e > 0) | (core == 0))
+                def _(slot=slot, to_z=to_z):
+                    send_k(slot, to_z * 8 + to_line, to_orb + 1)
+
+        return carry
+
+    lax.fori_loop(0, 16, spread_first, 0)
+
+    def spread_second(e, carry):
+        to_column, to_line, to_orb = column_at(e)
+        for n, to_turn in enumerate((7, 1, 5)):
+            to_z = lax.rem(to_turn + to_column, 8)
+
+            @pl.when((e > 0) | (core == 1) | (to_z != z))
+            def _(n=n, to_z=to_z):
+                send_k(128 + 16 * n + to_column, to_z * 8 + to_line, to_orb)
+
+        return carry
+
+    lax.fori_loop(0, 16, spread_second, 0)
+
+    def spread_late(e, carry):
+        place = lax.rem(e + column, 4)
+        to_column = 12 + place
+        to_z = lax.rem(6 + to_column, 8)
+
+        @pl.when((to_column != column) | (core == 1) | (to_z != z))
         def _():
-            remote(d_tiles.at[to_first], k_buf.at[me], s_k, r_k, to_ka, to_yh * 2 + 1).start()
-
-        @pl.when(there & ((d != 7) | (core == 1)))
-        def _():
-            remote(d_tiles.at[to_second], k_buf.at[me], s_k, r_k, to_ka, to_yh * 2).start()
+            send_k(164 + to_column, to_z * 8 + 6 + lax.rem(place, 2), 2 * lax.div(place, 2))
 
         return carry
 
-    lax.fori_loop(0, 128, spread_k, 0)
+    lax.fori_loop(0, 4, spread_late, 0)
     t_o, t_p = blocks_of(own_tile // 18)
     t_m = own_tile % 18
     mirrored = t_o != t_p
@@ -257,7 +303,7 @@
 
     @pl.when(has_tile)
     def _():
-        k_buf[me] = d_tiles[own_tile]
+        k_buf[me] = d_tiles[own_slot]
         wait_bytes(k_buf.at[pl.ds(0, K - 1)], r_k)
         k_rows = k_buf.reshape(K * 8, 128)
         o_rows = o_buf.reshape(2 * K * 8, 128)
@@ -279,24 +325,33 @@
 
         lax.fori_loop(0, 8, send_d0, 0)
 
-        def send_o(d, carry):
-            to_z = (z + far_then_near(d % 8)) % 8
-            to_x = (x + (d // 8) % 4) % 4
-            to_yl = (yl + d // 32) % 2
-            to_ka = to_z * 8 + to_x * 2 + to_yl
-            cells_at = pl.ds(4 * to_ka, 4)
-
-            @pl.when((d != 7) | (t_o != orb))
+        def send_o(e, carry):
+            to_x = lax.rem(x + lax.rem(e, 4), 4)
+            to_yl = lax.rem(yl + lax.div(e, 4), 2)
+            to_line = to_x * 2 + to_yl
+
+            def send_side(side, place, to_orb):
+                for step in STEPS:
+                    to_ka = lax.rem(z + step, 8) * 8 + to_line
+
+                    def send(to_ka=to_ka):
+                        cells_at = o_buf.at[side, pl.ds(4 * to_ka, 4)]
+                        remote(cells_at, landing.at[place], s_o, r_o, to_ka, to_orb).start()
+
+                    if step:
+                        send()
+                    else:
+                        pl.when((e > 0) | (to_orb != orb))(send)
+
+            send_side(0, t_p * 18 + t_m, t_o)
+
+            @pl.when(mirrored)
             def _():
-                remote(o_buf.at[0, cells_at], landing.at[t_p * 18 + t_m], s_o, r_o, to_ka, t_o).start()
-
-            @pl.when(mirrored & ((d != 7) | (t_p != orb)))
-            def _():
-                remote(o_buf.at[1, cells_at], landing.at[t_o * 18 + t_m], s_o, r_o, to_ka, t_p).start()
+                send_side(1, t_o * 18 + t_m, t_p)
 
             return carry
 
-        lax.fori_loop(0, 64, send_o, 0)
+        lax.fori_loop(0, 8, send_o, 0)
 
         @pl.when(t_o == orb)
         def _():
@@ -331,7 +386,7 @@
             f_out[part] = jnp.where(left, picked[:48], picked[48:96])
 
         def send_f(d, carry):
-            to_ka = ((z + far_then_near(d % 8)) % 8) * 8 + (ka + d // 8) % 8
+            to_ka = lax.rem(z + lax.rem(d * 3 + 4, 8), 8) * 8 + lax.rem(ka + lax.div(d, 8), 8)
             rows_at = pl.ds(pl.multiple_of(24 * f_half, 8), 24)
             remote(f_out.at[:, rows_at], f_in.at[:, rows_at], s_f, r_f, to_ka, f_o).start()
             return carry

time: 95.1 us -> 90.7 us (0.954)
  Pallas kernels: 92.8 us -> 88.4 us
    pallas_call x1, Pallas kernels: 74.8 us -> 70.4 us  [per_device(): pl.pallas_call(main_kernel, name='transform', out_shape=(jax.ShapeDtypeSt...]
where the time goes in v5:
time: 90.7 us; the launch traced here: 90.6 us
  Pallas kernels  88.4 us (97%)
  between operations  2.13 us (2%)
    pallas_call x1, Pallas kernels, per_device(): pl.pallas_call(main_kernel, name='transform', out_shape=(jax.ShapeDtypeSt...  70.4 us
    pallas_call x1, Pallas kernels, per_device(): pl.pallas_call(gather_kernel, name='gather', out_shape=jax.ShapeDtypeStru...  15 us
    pallas_call x1, Pallas kernels, per_device(): pl.pallas_call(store_kernel, name='store', out_shape=(jax.ShapeDtypeStruc...  3.02 us

profile of v5, /device:TPU:1, one launch (start us, length us, event | category | flops | bytes accessed | tf_op | source)
XLA Modules:
  0.0 90.6 jit_solution(8553173483712432181)
XLA Ops:
  1.9 0.0 copy-start
  1.9 0.0 copy-start.1
  1.9 15.0 %gather.1.x_in = f32[384,768]{1,0:T(8,128)S(1)} custom-call(f32[2,4,96,384]{3,2,1,0:T(8,128)} %fock_hbm.1, f32[48,48]{1,0:T(8,128)} %bitcast.3, f32[1]{0:T(128)S(6)} %copy.10.chem, f32[1]{0:T(128)S(6)} %copy.11.bound, s32[384]{0:T(512)} %imp_hbm.3, s32[8]{0:T(128)} %pof_hbm.1), custom_call_target="tpu_custom_call" | custom-call | tf_op jit(solution)/shard_map/gather/pallas_call | solution.py:480
  16.9 0.0 copy-done
  17.0 0.0 copy-done.1
  17.0 70.4 %transform.1 = (f32[72,4,8,128]{3,2,1,0:T(8,128)S(1)}, f32[2,48,128]{2,1,0:T(8,128)S(1)}) custom-call(f32[384,768]{1,0:T(8,128)S(1)} %gather.1.x_in, s32[384]{0:T(512)} %imp_hbm.3, bf16[512,256]{1,0:T(8,128)(2,1)S(1)} %copy-done.1, bf16[512,256]{1,0:T(8,128)(2,1)S(1)} %copy-done), custom_call_target="tpu_custom_call" | custom-call | tf_op jit(solution)/shard_map/transform/pallas_call | solution.py:508
  87.4 3.0 %store.1 = (f32[2,4,96,384]{3,2,1,0:T(8,128)}, f32[2,2,48,48]{3,2,1,0:T(8,128)}) custom-call(f32[72,4,8,128]{3,2,1,0:T(8,128)S(1)} %get-tuple-element.4.landing, f32[2,48,128]{2,1,0:T(8,128)S(1)} %get-tuple-element.5.f_in), custom_call_target="tpu_custom_call" | custom-call | tf_op jit(solution)/shard_map/store/pallas_call | solution.py:536
Async XLA Ops:
  1.9 15.0 %copy-start = (bf16[512,256]{1,0:T(8,128)(2,1)S(1)}, bf16[512,256]{1,0:T(8,128)(2,1)}, u32[]{:S(2)}) copy-start(bf16[512,256]{1,0:T(8,128)(2,1)} %constant.5.clone.t_lo) | copy-start | bytes 786436
  1.9 15.0 %copy-start.1 = (bf16[512,256]{1,0:T(8,128)(2,1)S(1)}, bf16[512,256]{1,0:T(8,128)(2,1)}, u32[]{:S(2)}) copy-start(bf16[512,256]{1,0:T(8,128)(2,1)} %constant.4.clone.t_hi) | copy-start | bytes 786436

commit v6 on v5

--- a/solution.py
+++ b/solution.py
@@ -114,6 +114,11 @@
 
 
 STEPS = (4, 3, 5, 2, 6, 1, 7, 0)
+
+
+def far_first(i):
+    half = lax.div(i, 2)
+    return (1 - half) * (2 + i) + half * (3 - i)
 
 
 def frag_device(g):
@@ -249,9 +254,9 @@
         remote(d_tiles.at[slot], k_buf.at[me], s_k, r_k, to_ka, to_orb).start()
 
     def column_at(e):
-        to_x = lax.rem(x + lax.rem(e, 4), 4)
-        to_yl = lax.rem(yl + lax.rem(lax.div(e, 4), 2), 2)
-        to_yh = lax.rem(yh + lax.div(e, 8), 2)
+        to_x = lax.rem(x + far_first(lax.rem(e, 4)), 4)
+        to_y = lax.rem(2 * yh + yl + far_first(lax.div(e, 4)), 4)
+        to_yh, to_yl = lax.div(to_y, 2), lax.rem(to_y, 2)
         return to_x * 4 + to_yh * 2 + to_yl, to_x * 2 + to_yl, to_yh * 2
 
     def spread_first(e, carry):
@@ -263,7 +268,7 @@
                 send_k(slot, to_z * 8 + to_line, to_orb + 1)
             else:
 
-                @pl.when((e > 0) | (core == 0))
+                @pl.when((e < 15) | (core == 0))
                 def _(slot=slot, to_z=to_z):
                     send_k(slot, to_z * 8 + to_line, to_orb + 1)
 
@@ -276,13 +281,11 @@
         for n, to_turn in enumerate((7, 1, 5)):
             to_z = lax.rem(to_turn + to_column, 8)
 
-            @pl.when((e > 0) | (core == 1) | (to_z != z))
+            @pl.when((e < 15) | (core == 1) | (to_z != z))
             def _(n=n, to_z=to_z):
                 send_k(128 + 16 * n + to_column, to_z * 8 + to_line, to_orb)
 
         return carry
-
-    lax.fori_loop(0, 16, spread_second, 0)
 
     def spread_late(e, carry):
         place = lax.rem(e + column, 4)
@@ -296,6 +299,7 @@
         return carry
 
     lax.fori_loop(0, 4, spread_late, 0)
+    lax.fori_loop(0, 16, spread_second, 0)
     t_o, t_p = blocks_of(own_tile // 18)
     t_m = own_tile % 18
     mirrored = t_o != t_p
@@ -326,8 +330,8 @@
         lax.fori_loop(0, 8, send_d0, 0)
 
         def send_o(e, carry):
-            to_x = lax.rem(x + lax.rem(e, 4), 4)
-            to_yl = lax.rem(yl + lax.div(e, 4), 2)
+            to_x = lax.rem(x + far_first(lax.rem(e, 4)), 4)
+            to_yl = lax.rem(yl + 1 - lax.div(e, 4), 2)
             to_line = to_x * 2 + to_yl
 
             def send_side(side, place, to_orb):
@@ -341,7 +345,7 @@
                     if step:
                         send()
                     else:
-                        pl.when((e > 0) | (to_orb != orb))(send)
+                        pl.when((e < 7) | (to_orb != orb))(send)
 
             send_side(0, t_p * 18 + t_m, t_o)
 

time: 90.7 us -> 90.2 us (level)
  no operation moved by 1% of the time
where the time goes in v6:
time: 90.2 us; the launch traced here: 90.1 us
  Pallas kernels  87.9 us (97%)
  between operations  2.13 us (2%)
    pallas_call x1, Pallas kernels, per_device(): pl.pallas_call(main_kernel, name='transform', out_shape=(jax.ShapeDtypeSt...  69.9 us
    pallas_call x1, Pallas kernels, per_device(): pl.pallas_call(gather_kernel, name='gather', out_shape=jax.ShapeDtypeStru...  15 us
    pallas_call x1, Pallas kernels, per_device(): pl.pallas_call(store_kernel, name='store', out_shape=(jax.ShapeDtypeStruc...  3.02 us

profile of v6, /device:TPU:1, one launch (start us, length us, event | category | flops | bytes accessed | tf_op | source)
XLA Modules:
  0.0 90.1 jit_solution(8614296703635962028)
XLA Ops:
  1.9 0.0 copy-start
  1.9 0.0 copy-start.1
  1.9 15.0 %gather.1.x_in = f32[384,768]{1,0:T(8,128)S(1)} custom-call(f32[2,4,96,384]{3,2,1,0:T(8,128)} %fock_hbm.1, f32[48,48]{1,0:T(8,128)} %bitcast.3, f32[1]{0:T(128)S(6)} %copy.10.chem, f32[1]{0:T(128)S(6)} %copy.11.bound, s32[384]{0:T(512)} %imp_hbm.3, s32[8]{0:T(128)} %pof_hbm.1), custom_call_target="tpu_custom_call" | custom-call | tf_op jit(solution)/shard_map/gather/pallas_call | solution.py:484
  16.9 0.0 copy-done
  17.0 0.0 copy-done.1
  17.0 69.9 %transform.1 = (f32[72,4,8,128]{3,2,1,0:T(8,128)S(1)}, f32[2,48,128]{2,1,0:T(8,128)S(1)}) custom-call(f32[384,768]{1,0:T(8,128)S(1)} %gather.1.x_in, s32[384]{0:T(512)} %imp_hbm.3, bf16[512,256]{1,0:T(8,128)(2,1)S(1)} %copy-done.1, bf16[512,256]{1,0:T(8,128)(2,1)S(1)} %copy-done), custom_call_target="tpu_custom_call" | custom-call | tf_op jit(solution)/shard_map/transform/pallas_call | solution.py:512
  86.9 3.0 %store.1 = (f32[2,4,96,384]{3,2,1,0:T(8,128)}, f32[2,2,48,48]{3,2,1,0:T(8,128)}) custom-call(f32[72,4,8,128]{3,2,1,0:T(8,128)S(1)} %get-tuple-element.4.landing, f32[2,48,128]{2,1,0:T(8,128)S(1)} %get-tuple-element.5.f_in), custom_call_target="tpu_custom_call" | custom-call | tf_op jit(solution)/shard_map/store/pallas_call | solution.py:540
Async XLA Ops:
  1.9 15.0 %copy-start = (bf16[512,256]{1,0:T(8,128)(2,1)S(1)}, bf16[512,256]{1,0:T(8,128)(2,1)}, u32[]{:S(2)}) copy-start(bf16[512,256]{1,0:T(8,128)(2,1)} %constant.5.clone.t_lo) | copy-start | bytes 786436
  1.9 15.0 %copy-start.1 = (bf16[512,256]{1,0:T(8,128)(2,1)S(1)}, bf16[512,256]{1,0:T(8,128)(2,1)}, u32[]{:S(2)}) copy-start(bf16[512,256]{1,0:T(8,128)(2,1)} %constant.4.clone.t_hi) | copy-start | bytes 786436

commit v7 on v6

--- a/solution.py
+++ b/solution.py
@@ -122,8 +122,8 @@
 
 
 def frag_device(g):
-    column = (g + 6) % 8
-    return 8 * g + 2 * (column // 4) + column % 2, 2 * ((column // 2) % 2)
+    z = lax.rem(g + 3, 8)
+    return 8 * z + 2 * lax.div(g, 4) + lax.rem(g, 2), 2 * lax.rem(lax.div(g, 2), 2)
 
 
 def gather_kernel(
@@ -327,7 +327,7 @@
             remote(o_buf.at[0, 0], d0_buf.at[own_tile], s_d0, r_d0, to_ka, to_orb).start()
             return carry
 
-        lax.fori_loop(0, 8, send_d0, 0)
+        lax.fori_loop(0, 12, send_d0, 0)
 
         def send_o(e, carry):
             to_x = lax.rem(x + far_first(lax.rem(e, 4)), 4)
@@ -365,8 +365,8 @@
         def _():
             landing[t_o * 18 + t_m] = o_buf[1, pl.ds(4 * ka, 4)]
 
-    f_o, f_half = z % 4, z // 4
-    makes = (core == 0) & (column == (z + 6) % 8)
+    f_o, f_part = lax.rem(column + 1, 4), lax.div(column, 4)
+    makes = (core == 0) & (turn == 3) & (column < 12)
 
     @pl.when(makes)
     def _():
@@ -391,7 +391,7 @@
 
         def send_f(d, carry):
             to_ka = lax.rem(z + lax.rem(d * 3 + 4, 8), 8) * 8 + lax.rem(ka + lax.div(d, 8), 8)
-            rows_at = pl.ds(pl.multiple_of(24 * f_half, 8), 24)
+            rows_at = pl.ds(pl.multiple_of(16 * f_part, 8), 16)
             remote(f_out.at[:, rows_at], f_in.at[:, rows_at], s_f, r_f, to_ka, f_o).start()
             return carry
 
@@ -411,7 +411,7 @@
     @pl.when(has_tile)
     def _():
         wait_bytes(d_tiles.at[pl.ds(0, TILES - 1)], s_k)
-        wait_bytes(d_tiles.at[pl.ds(0, 8)], s_d0)
+        wait_bytes(d_tiles.at[pl.ds(0, 12)], s_d0)
 
     @pl.when(jnp.logical_not(has_tile))
     def _():
@@ -432,7 +432,7 @@
 
     @pl.when(makes)
     def _():
-        wait_bytes(o_buf.at[:, pl.ds(0, 192)], s_f)
+        wait_bytes(k_buf, s_f)
 
 
 def store_kernel(landing, f_in, out, frag, buf, sem):

time: 90.2 us -> 86.3 us (0.957)
  Pallas kernels: 87.9 us -> 83.7 us
    pallas_call x1, Pallas kernels: 69.9 us -> 65.7 us  [per_device(): pl.pallas_call(main_kernel, name='transform', out_shape=(jax.ShapeDtypeSt...]
where the time goes in v7:
time: 86.3 us; the launch traced here: 85.8 us
  Pallas kernels  83.7 us (97%)
  between operations  2.13 us (2%)
    pallas_call x1, Pallas kernels, per_device(): pl.pallas_call(main_kernel, name='transform', out_shape=(jax.ShapeDtypeSt...  65.7 us
    pallas_call x1, Pallas kernels, per_device(): pl.pallas_call(gather_kernel, name='gather', out_shape=jax.ShapeDtypeStru...  15 us
    pallas_call x1, Pallas kernels, per_device(): pl.pallas_call(store_kernel, name='store', out_shape=(jax.ShapeDtypeStruc...  3.02 us

profile of v7, /device:TPU:1, one launch (start us, length us, event | category | flops | bytes accessed | tf_op | source)
XLA Modules:
  0.0 85.8 jit_solution(5300419641756751137)
XLA Ops:
  1.9 0.0 copy-start
  1.9 0.0 copy-start.1
  1.9 15.0 %gather.1.x_in = f32[384,768]{1,0:T(8,128)S(1)} custom-call(f32[2,4,96,384]{3,2,1,0:T(8,128)} %fock_hbm.1, f32[48,48]{1,0:T(8,128)} %bitcast.3, f32[1]{0:T(128)S(6)} %copy.10.chem, f32[1]{0:T(128)S(6)} %copy.11.bound, s32[384]{0:T(512)} %imp_hbm.3, s32[8]{0:T(128)} %pof_hbm.1), custom_call_target="tpu_custom_call" | custom-call | tf_op jit(solution)/shard_map/gather/pallas_call | solution.py:484
  16.9 0.0 copy-done
  17.0 0.0 copy-done.1
  17.0 65.7 %transform.1 = (f32[72,4,8,128]{3,2,1,0:T(8,128)S(1)}, f32[2,48,128]{2,1,0:T(8,128)S(1)}) custom-call(f32[384,768]{1,0:T(8,128)S(1)} %gather.1.x_in, s32[384]{0:T(512)} %imp_hbm.3, bf16[512,256]{1,0:T(8,128)(2,1)S(1)} %copy-done.1, bf16[512,256]{1,0:T(8,128)(2,1)S(1)} %copy-done), custom_call_target="tpu_custom_call" | custom-call | tf_op jit(solution)/shard_map/transform/pallas_call | solution.py:512
  82.6 3.0 %store.1 = (f32[2,4,96,384]{3,2,1,0:T(8,128)}, f32[2,2,48,48]{3,2,1,0:T(8,128)}) custom-call(f32[72,4,8,128]{3,2,1,0:T(8,128)S(1)} %get-tuple-element.4.landing, f32[2,48,128]{2,1,0:T(8,128)S(1)} %get-tuple-element.5.f_in), custom_call_target="tpu_custom_call" | custom-call | tf_op jit(solution)/shard_map/store/pallas_call | solution.py:540
Async XLA Ops:
  1.9 15.0 %copy-start = (bf16[512,256]{1,0:T(8,128)(2,1)S(1)}, bf16[512,256]{1,0:T(8,128)(2,1)}, u32[]{:S(2)}) copy-start(bf16[512,256]{1,0:T(8,128)(2,1)} %constant.5.clone.t_lo) | copy-start | bytes 786436
  1.9 15.0 %copy-start.1 = (bf16[512,256]{1,0:T(8,128)(2,1)S(1)}, bf16[512,256]{1,0:T(8,128)(2,1)}, u32[]{:S(2)}) copy-start(bf16[512,256]{1,0:T(8,128)(2,1)} %constant.4.clone.t_hi) | copy-start | bytes 786436

commit v8 on v7

--- a/solution.py
+++ b/solution.py
@@ -138,21 +138,33 @@
     loads = [
         pltpu.make_async_copy(source, target, s_in.at[n])
         for n, (source, target) in enumerate(
-            ((fock_hbm, fock), (pot_hbm, pot), (imp_hbm, imp_flat), (pof_hbm, pof))
+            ((pot_hbm, pot), (imp_hbm, imp_flat), (pof_hbm, pof))
         )
     ]
+    parts = {}
+    for n, step in enumerate((2, 3, 1, 0)):
+        to = (orb + step) % 4
+        parts[step] = pltpu.make_async_copy(fock_hbm.at[:, to], fock.at[:, to], s_in.at[3 + n])
+        parts[step].start()
     for load in loads:
         load.start()
+    def add(step):
+        to = (orb + step) % 4
+        parts[step].wait()
+        m_src[to] = fock[0, to] + fock[1, to]
+
+    add(2)
+    pl.semaphore_wait(barrier, 3)
+    for step in (2, 3, 1):
+        if step != 2:
+            add(step)
+        to = (orb + step) % 4
+        remote(m_src.at[to], m_all.at[orb], s_fock.at[step], r_fock.at[step], ka, to).start()
     for load in loads:
         load.wait()
-    m_src[...] = fock[0] + fock[1]
-    pl.semaphore_wait(barrier, 3)
     for step in (2, 3, 1):
-        to = (orb + step) % 4
-        remote(pot, pot_all.at[orb], s_pot.at[step], r_pot.at[step], ka, to).start()
-    for step in (2, 3, 1):
-        to = (orb + step) % 4
-        remote(m_src.at[to], m_all.at[orb], s_fock.at[step], r_fock.at[step], ka, to).start()
+        remote(pot, pot_all.at[orb], s_pot.at[step], r_pot.at[step], ka, (orb + step) % 4).start()
+    add(0)
     pot_all[orb] = pot[...]
     m_all[orb] = m_src[orb]
 
@@ -496,7 +508,7 @@
             pltpu.VMEM((4, 96, N), F32),
             pltpu.VMEM((4, 48, 48), F32),
             pltpu.VMEM((N, N), F32),
-            dma((4,)), dma((4,)), dma((4,)), dma((4,)), dma((4,)),
+            dma((7,)), dma((4,)), dma((4,)), dma((4,)), dma((4,)),
         ],
         compiler_params=pltpu.CompilerParams(
             has_side_effects=True, collective_id=0, vmem_limit_bytes=40 << 20

time: 86.3 us -> 91.5 us (1.060)
  Pallas kernels: 83.7 us -> 89.2 us
    pallas_call x1, Pallas kernels: 15 us -> 19.2 us  [per_device(): pl.pallas_call(gather_kernel, name='gather', out_shape=jax.ShapeDtypeStru...]
    pallas_call x1, Pallas kernels: 65.7 us -> 67 us  [per_device(): pl.pallas_call(main_kernel, name='transform', out_shape=(jax.ShapeDtypeSt...]
where the time goes in v8:
time: 91.5 us; the launch traced here: 91.3 us
  Pallas kernels  89.2 us (97%)
  between operations  2.13 us (2%)
    pallas_call x1, Pallas kernels, per_device(): pl.pallas_call(main_kernel, name='transform', out_shape=(jax.ShapeDtypeSt...  67 us
    pallas_call x1, Pallas kernels, per_device(): pl.pallas_call(gather_kernel, name='gather', out_shape=jax.ShapeDtypeStru...  19.2 us
    pallas_call x1, Pallas kernels, per_device(): pl.pallas_call(store_kernel, name='store', out_shape=(jax.ShapeDtypeStruc...  3.02 us

profile of v8, /device:TPU:1, one launch (start us, length us, event | category | flops | bytes accessed | tf_op | source)
XLA Modules:
  0.0 91.3 jit_solution(16410457492454418343)
XLA Ops:
  1.9 0.0 copy-start
  1.9 0.0 copy-start.1
  1.9 19.2 %gather.1.x_in = f32[384,768]{1,0:T(8,128)S(1)} custom-call(f32[2,4,96,384]{3,2,1,0:T(8,128)} %fock_hbm.1, f32[48,48]{1,0:T(8,128)} %bitcast.3, f32[1]{0:T(128)S(6)} %copy.10.chem, f32[1]{0:T(128)S(6)} %copy.11.bound, s32[384]{0:T(512)} %imp_hbm.3, s32[8]{0:T(128)} %pof_hbm.1), custom_call_target="tpu_custom_call" | custom-call | tf_op jit(solution)/shard_map/gather/pallas_call | solution.py:496
  21.1 0.0 copy-done
  21.1 0.0 copy-done.1
  21.2 67.0 %transform.1 = (f32[72,4,8,128]{3,2,1,0:T(8,128)S(1)}, f32[2,48,128]{2,1,0:T(8,128)S(1)}) custom-call(f32[384,768]{1,0:T(8,128)S(1)} %gather.1.x_in, s32[384]{0:T(512)} %imp_hbm.3, bf16[512,256]{1,0:T(8,128)(2,1)S(1)} %copy-done.1, bf16[512,256]{1,0:T(8,128)(2,1)S(1)} %copy-done), custom_call_target="tpu_custom_call" | custom-call | tf_op jit(solution)/shard_map/transform/pallas_call | solution.py:524
  88.2 3.0 %store.1 = (f32[2,4,96,384]{3,2,1,0:T(8,128)}, f32[2,2,48,48]{3,2,1,0:T(8,128)}) custom-call(f32[72,4,8,128]{3,2,1,0:T(8,128)S(1)} %get-tuple-element.4.landing, f32[2,48,128]{2,1,0:T(8,128)S(1)} %get-tuple-element.5.f_in), custom_call_target="tpu_custom_call" | custom-call | tf_op jit(solution)/shard_map/store/pallas_call | solution.py:552
Async XLA Ops:
  1.9 19.2 %copy-start = (bf16[512,256]{1,0:T(8,128)(2,1)S(1)}, bf16[512,256]{1,0:T(8,128)(2,1)}, u32[]{:S(2)}) copy-start(bf16[512,256]{1,0:T(8,128)(2,1)} %constant.5.clone.t_lo) | copy-start | bytes 786436
  1.9 19.2 %copy-start.1 = (bf16[512,256]{1,0:T(8,128)(2,1)S(1)}, bf16[512,256]{1,0:T(8,128)(2,1)}, u32[]{:S(2)}) copy-start(bf16[512,256]{1,0:T(8,128)(2,1)} %constant.4.clone.t_hi) | copy-start | bytes 786436
